TPU v7x, 256 devices: a whole 4x4x8 slice. The times are simulated.
256 devices in a mesh: inl: 8 (over z), xln: 32 (over y, x, core).
Axes of the slice: x: 4, y: 4, z: 8, core: 2. Of those that a mesh axis runs over, the one named last changes fastest.
Arguments:
- noisy: float32 [256, 1024, 512], P('inl', 'xln'), may hold values from -6 to 6
- bound: float32 [256, 1024, 512], P('inl', 'xln'), may hold values from 0.05 to 0.5
Outputs:
- denoised: float32 [256, 1024, 512], P('inl', 'xln')
- dual: float32 [3, 256, 1024, 512], P(None, 'inl', 'xln')
- norms: float32 [2, 2], replicated
All inputs are finite; a program needn't handle non-finite values.
Results may differ from a plain program's by a relative error of at most 0.0001.
Values sent between devices are 32-bit elements; how exact they have to be, the bound alone decides.
No kernel may reach another device: no remote copies, remote signals or barrier semaphores. Data moves between devices by JAX's collectives and lax.ppermute only.
A program may use at most 64 MiB of HBM per device.

v0:
```python
import functools

import jax
import jax.numpy as jnp
from jax import lax
from jax.sharding import Mesh
from jax.sharding import PartitionSpec as P

ITERS = 2
INL_XLN = ("inl", "xln_0", "xln_1", "xln_2")
XLN = ("xln_0", "xln_1", "xln_2")


SIGMA = 0.28
TAU = 0.28


def over_axes(shard, axes):
    return functools.reduce(lax.psum, axes, shard)


def passed_along(value, axis, steps):
    count = lax.axis_size(axis)
    first, last = (max(0, -steps), min(count, count - steps))
    return lax.ppermute(value, axis, [(source, source + steps) for source in range(first, last)])


def depth_forward(field):
    return jnp.concatenate(
        [field[:, :, 1:] - field[:, :, :-1], jnp.zeros_like(field[:, :, :1])], axis=2
    )


def depth_backward(field):
    return field - jnp.concatenate([jnp.zeros_like(field[:, :, :1]), field[:, :, :-1]], axis=2)


def finish(rows):
    return jnp.stack(rows)


def record(primal_sum, dual_sum, rows):
    total_p, total_d = (over_axes(primal_sum, INL_XLN), over_axes(dual_sum, INL_XLN))
    rows.append(jnp.sqrt(jnp.stack([total_p, total_d])))


def per_device(noisy, bound):
    rows = []
    inl_flag = (lax.axis_index("inl") < lax.axis_size("inl") - 1).astype(jnp.float32)
    xln_flag = (lax.axis_index(XLN) < lax.axis_size(XLN) - 1).astype(jnp.float32)
    primal = noisy
    smooth = noisy
    dual_i = jnp.zeros_like(noisy)
    dual_x = jnp.zeros_like(noisy)
    dual_z = jnp.zeros_like(noisy)
    for step in range(ITERS):
        next_i = passed_along(smooth[0:1], "inl", -1)
        next_x = passed_along(smooth[:, 0:1], XLN, -1)
        grad_i = jnp.concatenate(
            [smooth[1:] - smooth[:-1], (next_i - smooth[-1:]) * inl_flag], axis=0
        )
        grad_x = jnp.concatenate(
            [smooth[:, 1:] - smooth[:, :-1], (next_x - smooth[:, -1:]) * xln_flag], axis=1
        )
        fresh_i = jnp.clip(dual_i + SIGMA * grad_i, -bound, bound)
        fresh_x = jnp.clip(dual_x + SIGMA * grad_x, -bound, bound)
        fresh_z = jnp.clip(dual_z + SIGMA * depth_forward(smooth), -bound, bound)
        prev_i = passed_along(fresh_i[-1:], "inl", 1)
        prev_x = passed_along(fresh_x[:, -1:], XLN, 1)
        diverge = fresh_i - jnp.concatenate([prev_i, fresh_i[:-1]], axis=0)
        diverge = diverge + (fresh_x - jnp.concatenate([prev_x, fresh_x[:, :-1]], axis=1))
        diverge = diverge + depth_backward(fresh_z)
        updated = (primal + TAU * diverge + TAU * noisy) / (1.0 + TAU)
        primal_sum = jnp.sum((updated - primal) ** 2)
        dual_sum = (
            jnp.sum((fresh_i - dual_i) ** 2)
            + jnp.sum((fresh_x - dual_x) ** 2)
            + jnp.sum((fresh_z - dual_z) ** 2)
        )
        record(primal_sum, dual_sum, rows)
        smooth = 2.0 * updated - primal
        primal = updated
        dual_i, dual_x, dual_z = (fresh_i, fresh_x, fresh_z)
    norms = finish(rows)
    return (primal, jnp.stack([dual_i, dual_x, dual_z]), norms)


def solution(mesh):
    split = Mesh(
        mesh.devices.reshape(mesh.shape["inl"], 4, 4, 2), ("inl", "xln_0", "xln_1", "xln_2")
    )
    in_specs = (P("inl", XLN, None), P("inl", XLN, None))
    out_specs = (P("inl", XLN, None), P(None, "inl", XLN, None), P())
    return jax.shard_map(
        per_device, mesh=split, in_specs=in_specs, out_specs=out_specs, check_vma=False
    )
```

profile of v0, /device:TPU:1, one launch (start us, length us, event | category | flops | bytes accessed | tf_op | source)
XLA Modules:
  0.0 118.3 jit_solution(15434490687929632342)
XLA Ops:
  1.5 1.3 %collective-permute-start = (f32[1,32,512]{2,1,0:T(8,128)S(1)}, f32[1,32,512]{2,1,0:T(8,128)S(1)}, u32[]{:S(2)}, u32[]{:S(2)}) collective-permute-start(f32[1,32,512]{2,1,0:T(8,128)S(1)} %slice.92), channel_id=1, source_target_pairs={{32,0},{64,32},{96,64},{128,96},{160,128},{192,160},{224,192},{33,... | collective-permute-start | bytes 196616 | tf_op jit(solution)/shard_map/ppermute | solution.py:25
  2.8 1.1 slice.98
  3.9 5.2 %collective-permute-start.2 = (f32[32,1,512]{2,1,0:T(1,128)S(1)}, f32[32,1,512]{2,1,0:T(1,128)S(1)}, u32[]{:S(2)}, u32[]{:S(2)}) collective-permute-start(f32[32,1,512]{2,1,0:T(1,128)S(1)} %slice.98), channel_id=1, source_target_pairs={{1,0},{2,1},{3,2},{4,3},{5,4},{6,5},{7,6},{8,7},{9,8},{10,9},{11,1... | collective-permute-start | bytes 196616 | tf_op jit(solution)/shard_map/ppermute | solution.py:25
  9.1 4.1 %slice_subtract_fusion.3 = f32[32,31,512]{2,1,0:T(8,128)} fusion(f32[32,32,512]{2,1,0:T(8,128)} %param.2), kind=kLoop, calls=%fused_computation.44 | loop fusion | flops 507904 | bytes 6094848 | tf_op jit(solution)/shard_map/sub | solution.py:63
  13.2 2.0 %slice_subtract_fusion.2 = f32[32,32,511]{2,1,0:T(8,128)} fusion(f32[32,32,512]{2,1,0:T(8,128)S(1)} %copy-done), kind=kLoop, calls=%fused_computation.43 | loop fusion | flops 523264 | bytes 6279168 | tf_op jit(solution)/shard_map/sub | solution.py:30
  15.2 1.7 %slice_subtract_fusion.5 = f32[31,32,512]{2,1,0:T(8,128)} fusion(f32[32,32,512]{2,1,0:T(8,128)S(1)} %copy-done), kind=kLoop, calls=%fused_computation.46 | loop fusion | flops 507904 | bytes 6094848 | tf_op jit(solution)/shard_map/sub | solution.py:60
  16.9 4.5 %fusion.1 = (f32[32,32,512]{2,1,0:T(8,128)S(1)}, f32[32,32,512]{2,1,0:T(8,128)S(1)}, f32[32,32,512]{2,1,0:T(8,128)S(1)}) fusion(f32[32,32,512]{2,1,0:T(8,128)} %param.3, f32[1,32,512]{2,1,0:T(8,128)S(1)} %subtract_multiply_fusion.1, f32[31,32,512]{2,1,0:T(8,128)} %slice_subtract_fusion.5, f32[32,32,511]{2,1,0:T(8,128)} %slice_subtract_fusion.2, ...), kind=kLoop, calls=%fused_computation.5 | loop fusion | flops 6291456 | bytes 14675968 | tf_op jit(solution)/shard_map/jit(clip)/min | solution.py:65
  21.6 1.9 %collective-permute-start.3 = (f32[32,1,512]{2,1,0:T(1,128)S(1)}, f32[32,1,512]{2,1,0:T(1,128)S(1)}, u32[]{:S(2)}, u32[]{:S(2)}) collective-permute-start(f32[32,1,512]{2,1,0:T(1,128)S(1)} %slice.122), channel_id=1, source_target_pairs={{0,1},{1,2},{2,3},{3,4},{4,5},{5,6},{6,7},{7,8},{8,9},{9,10},{10,1... | collective-permute-start | bytes 196616 | tf_op jit(solution)/shard_map/ppermute | solution.py:25
  23.5 4.3 %collective-permute-start.1 = (f32[1,32,512]{2,1,0:T(8,128)S(1)}, f32[1,32,512]{2,1,0:T(8,128)S(1)}, u32[]{:S(2)}, u32[]{:S(2)}) collective-permute-start(f32[1,32,512]{2,1,0:T(8,128)S(1)} %slice.120), channel_id=1, source_target_pairs={{0,32},{32,64},{64,96},{96,128},{128,160},{160,192},{192,224},{1,3... | collective-permute-start | bytes 196616 | tf_op jit(solution)/shard_map/ppermute | solution.py:25
  29.1 3.5 %multiply_subtract_fusion = (f32[32,32,512]{2,1,0:T(8,128)S(1)}, f32[32,32,512]{2,1,0:T(8,128)}) fusion(f32[32,32,512]{2,1,0:T(8,128)S(1)} %copy-done, f32[32,32,512]{2,1,0:T(8,128)S(1)} %get-tuple-element.40, f32[32,32,511]{2,1,0:T(8,128)S(1)} %bitcast.14, f32[32,32,512]{2,1,0:T(8,128)S(1)} %get-tuple-element.41, f32[32,31,512]{2,1,0:T(8,128)S(1)} %bitcast.11, ...), kind=kLoop, calls=%fused_computation.41 | loop fusion | flops 6815744 | bytes 18870272 | tf_op jit(solution)/shard_map/sub | solution.py:81
  33.5 1.4 %collective-permute-start.4 = (f32[1,32,512]{2,1,0:T(8,128)S(1)}, f32[1,32,512]{2,1,0:T(8,128)S(1)}, u32[]{:S(2)}, u32[]{:S(2)}) collective-permute-start(f32[1,32,512]{2,1,0:T(8,128)S(1)} %slice.127), channel_id=1, source_target_pairs={{32,0},{64,32},{96,64},{128,96},{160,128},{192,160},{224,192},{33,... | collective-permute-start | bytes 196616 | tf_op jit(solution)/shard_map/ppermute | solution.py:25
  35.3 3.3 %collective-permute-start.6 = (f32[32,1,512]{2,1,0:T(1,128)S(1)}, f32[32,1,512]{2,1,0:T(1,128)S(1)}, u32[]{:S(2)}, u32[]{:S(2)}) collective-permute-start(f32[32,1,512]{2,1,0:T(1,128)S(1)} %slice.133), channel_id=1, source_target_pairs={{1,0},{2,1},{3,2},{4,3},{5,4},{6,5},{7,6},{8,7},{9,8},{10,9},{11,1... | collective-permute-start | bytes 196616 | tf_op jit(solution)/shard_map/ppermute | solution.py:25
  39.0 2.1 %collective-permute-done.6 = f32[32,1,512]{2,1,0:T(1,128)S(1)} collective-permute-done((f32[32,1,512]{2,1,0:T(1,128)S(1)}, f32[32,1,512]{2,1,0:T(1,128)S(1)}, u32[]{:S(2)}, u32[]{:S(2)}) %collective-permute-start.6) | collective-permute-done | bytes 65568 | tf_op jit(solution)/shard_map/ppermute | solution.py:25
  41.2 2.9 %multiply_reduce_fusion.6 = (f32[]{:T(128)}, f32[]{:T(128)}, f32[32,32,512]{2,1,0:T(8,128)S(1)}, f32[]{:T(128)}, f32[32,32,512]{2,1,0:T(8,128)S(1)}, /*index=5*/...) fusion(f32[32,32,512]{2,1,0:T(8,128)S(1)} %get-tuple-element.39, f32[32,32,512]{2,1,0:T(8,128)S(1)} %copy-done.4, ...), kind=kLoop, calls=%fused_computation.38 | loop fusion | flops 15728634 | bytes 20967448 | tf_op jit(solution)/shard_map/reduce_sum | solution.py:76
  44.2 2.4 %collective-permute-start.7 = (f32[32,1,512]{2,1,0:T(1,128)S(1)}, f32[32,1,512]{2,1,0:T(1,128)S(1)}, u32[]{:S(2)}, u32[]{:S(2)}) collective-permute-start(f32[32,1,512]{2,1,0:T(1,128)S(1)} %slice.135), channel_id=1, source_target_pairs={{0,1},{1,2},{2,3},{3,4},{4,5},{5,6},{6,7},{7,8},{8,9},{9,10},{10,1... | collective-permute-start | bytes 196616 | tf_op jit(solution)/shard_map/ppermute | solution.py:25
  46.6 3.6 %collective-permute-start.5 = (f32[1,32,512]{2,1,0:T(8,128)S(1)}, f32[1,32,512]{2,1,0:T(8,128)S(1)}, u32[]{:S(2)}, u32[]{:S(2)}) collective-permute-start(f32[1,32,512]{2,1,0:T(8,128)S(1)} %slice.129), channel_id=1, source_target_pairs={{0,32},{32,64},{64,96},{96,128},{128,160},{160,192},{192,224},{1,3... | collective-permute-start | bytes 196616 | tf_op jit(solution)/shard_map/ppermute | solution.py:25
  50.2 3.4 %pad_maximum_fusion = f32[3,32,32,512]{3,2,1,0:T(8,128)} fusion(f32[1,32,32,512]{3,2,1,0:T(8,128)S(1)} %bitcast.15, f32[1,32,32,512]{3,2,1,0:T(8,128)S(1)} %bitcast.12, f32[1,32,32,512]{3,2,1,0:T(8,128)S(1)} %bitcast.17), kind=kLoop, calls=%fused_computation | loop fusion | flops 3145728 | bytes 12582912 | tf_op jit(solution)/shard_map/stack | solution.py:85
  53.6 1.5 %slice.130 = f32[31,32,512]{2,1,0:T(8,128)} slice(f32[32,32,512]{2,1,0:T(8,128)S(1)} %get-tuple-element.30), slice={[0:31], [0:32], [0:512]} | slice | bytes 4063232 | tf_op jit(solution)/shard_map/slice | solution.py:70
  58.8 8.1 %multiply_reduce_fusion.7 = (f32[]{:T(128)}, f32[]{:T(128)}, f32[32,32,512]{2,1,0:T(8,128)}) fusion(f32[32,32,512]{2,1,0:T(8,128)S(1)} %copy-done, f32[32,32,512]{2,1,0:T(8,128)} %get-tuple-element.32, f32[32,32,512]{2,1,0:T(8,128)} %copy-done.2, f32[32,32,511]{2,1,0:T(8,128)} %bitcast.16, f32[32,32,512]{2,1,0:T(8,128)} %copy-done.1, ...), kind=kLoop, calls=%fused_computation.39 | loop fusion | flops 9961470 | bytes 18870280 | tf_op jit(solution)/shard_map/reduce_sum | solution.py:74
  66.9 16.6 %all-reduce.4 = (f32[]{:T(128)}, f32[]{:T(128)}, f32[]{:T(128)}, f32[]{:T(128)}) all-reduce(f32[]{:T(128)S(6)} %add.107, f32[]{:T(128)} %get-tuple-element.4, f32[]{:T(128)S(6)} %add.105, f32[]{:T(128)} %get-tuple-element.3), channel_id=1, replica_groups=mesh['inl'=8,'xln_0'=4,'xln_1'=4,'xln_2'=2] {'inl'}, use_global_device_ids=true, to_apply=%region_20.21 | all-reduce | flops 4 | bytes 32 | tf_op jit(solution)/shard_map/psum | solution.py:19
  83.5 9.7 %all-reduce.6 = (f32[]{:T(128)}, f32[]{:T(128)}, f32[]{:T(128)}, f32[]{:T(128)}) all-reduce(f32[]{:T(128)} %get-tuple-element.11, f32[]{:T(128)} %get-tuple-element.12, f32[]{:T(128)} %get-tuple-element.13, f32[]{:T(128)} %get-tuple-element.14), channel_id=1, replica_groups=mesh['inl'=8,'xln_0'=4,'xln_1'=4,'xln_2'=2] {'xln_0'}, use_global_device_ids=true, to_apply=%region_21.22 | all-reduce | flops 4 | bytes 32 | tf_op jit(solution)/shard_map/psum | solution.py:19
  93.2 10.6 %all-reduce.5 = (f32[]{:T(128)}, f32[]{:T(128)}, f32[]{:T(128)}, f32[]{:T(128)}) all-reduce(f32[]{:T(128)} %get-tuple-element.19, f32[]{:T(128)} %get-tuple-element.20, f32[]{:T(128)} %get-tuple-element.21, f32[]{:T(128)} %get-tuple-element.22), channel_id=1, replica_groups=mesh['inl'=8,'xln_0'=4,'xln_1'=4,'xln_2'=2] {'xln_1'}, use_global_device_ids=true, to_apply=%region_22.23 | all-reduce | flops 4 | bytes 32 | tf_op jit(solution)/shard_map/psum | solution.py:19
  103.8 11.4 %all-reduce.7 = (f32[1,1]{1,0:T(1,128)}, f32[1,1]{1,0:T(1,128)}, f32[1,1]{1,0:T(1,128)}, f32[1,1]{1,0:T(1,128)}) all-reduce(f32[1,1]{1,0:T(1,128)} %bitcast.6, f32[1,1]{1,0:T(1,128)} %bitcast.5, f32[1,1]{1,0:T(1,128)} %bitcast.4, f32[1,1]{1,0:T(1,128)} %bitcast.3), channel_id=1, replica_groups=mesh['inl'=8,'xln_0'=4,'xln_1'=4,'xln_2'=2] {'xln_2'}, use_global_device_ids=true, to_apply=%region_23.24 | all-reduce | flops 4 | bytes 32 | tf_op jit(solution)/shard_map/psum | solution.py:19
  115.2 2.6 %maximum_sqrt_fusion = (f32[1,2]{1,0:T(1,128)S(1)}, f32[1,2]{1,0:T(1,128)S(1)}) fusion(f32[1,1]{1,0:T(1,128)} %get-tuple-element.25, f32[1,1]{1,0:T(1,128)} %get-tuple-element.26, f32[1,1]{1,0:T(1,128)} %get-tuple-element.23, f32[1,1]{1,0:T(1,128)} %get-tuple-element.24), kind=kLoop, calls=%fused_computation.54 | loop fusion | flops 4 | bytes 32 | tf_op jit(solution)/shard_map/sqrt | solution.py:44
  (33 shorter events, 4.8 us)
Async XLA Ops:
  1.5 15.3 %collective-permute-start = (f32[1,32,512]{2,1,0:T(8,128)S(1)}, f32[1,32,512]{2,1,0:T(8,128)S(1)}, u32[]{:S(2)}, u32[]{:S(2)}) collective-permute-start(f32[1,32,512]{2,1,0:T(8,128)S(1)} %slice.92), channel_id=1, source_target_pairs={{32,0},{64,32},{96,64},{128,96},{160,128},{192,160},{224,192},{33,... | collective-permute-start | bytes 196616 | tf_op jit(solution)/shard_map/ppermute | solution.py:25
  3.8 9.3 %copy-start = (f32[32,32,512]{2,1,0:T(8,128)S(1)}, f32[32,32,512]{2,1,0:T(8,128)}, u32[]{:S(2)}) copy-start(f32[32,32,512]{2,1,0:T(8,128)} %param.2) | copy-start | bytes 6291460
  3.9 13.0 %collective-permute-start.2 = (f32[32,1,512]{2,1,0:T(1,128)S(1)}, f32[32,1,512]{2,1,0:T(1,128)S(1)}, u32[]{:S(2)}, u32[]{:S(2)}) collective-permute-start(f32[32,1,512]{2,1,0:T(1,128)S(1)} %slice.98), channel_id=1, source_target_pairs={{1,0},{2,1},{3,2},{4,3},{5,4},{6,5},{7,6},{8,7},{9,8},{10,9},{11,1... | collective-permute-start | bytes 196616 | tf_op jit(solution)/shard_map/ppermute | solution.py:25
  21.6 6.5 %collective-permute-start.3 = (f32[32,1,512]{2,1,0:T(1,128)S(1)}, f32[32,1,512]{2,1,0:T(1,128)S(1)}, u32[]{:S(2)}, u32[]{:S(2)}) collective-permute-start(f32[32,1,512]{2,1,0:T(1,128)S(1)} %slice.122), channel_id=1, source_target_pairs={{0,1},{1,2},{2,3},{3,4},{4,5},{5,6},{6,7},{7,8},{8,9},{9,10},{10,1... | collective-permute-start | bytes 196616 | tf_op jit(solution)/shard_map/ppermute | solution.py:25
  23.5 5.6 %collective-permute-start.1 = (f32[1,32,512]{2,1,0:T(8,128)S(1)}, f32[1,32,512]{2,1,0:T(8,128)S(1)}, u32[]{:S(2)}, u32[]{:S(2)}) collective-permute-start(f32[1,32,512]{2,1,0:T(8,128)S(1)} %slice.120), channel_id=1, source_target_pairs={{0,32},{32,64},{64,96},{96,128},{128,160},{160,192},{192,224},{1,3... | collective-permute-start | bytes 196616 | tf_op jit(solution)/shard_map/ppermute | solution.py:25
  33.5 7.7 %copy-start.4 = (f32[32,32,512]{2,1,0:T(8,128)S(1)}, f32[32,32,512]{2,1,0:T(8,128)}, u32[]{:S(2)}) copy-start(f32[32,32,512]{2,1,0:T(8,128)} %param.3) | copy-start | bytes 6291460
  33.5 5.5 %collective-permute-start.4 = (f32[1,32,512]{2,1,0:T(8,128)S(1)}, f32[1,32,512]{2,1,0:T(8,128)S(1)}, u32[]{:S(2)}, u32[]{:S(2)}) collective-permute-start(f32[1,32,512]{2,1,0:T(8,128)S(1)} %slice.127), channel_id=1, source_target_pairs={{32,0},{64,32},{96,64},{128,96},{160,128},{192,160},{224,192},{33,... | collective-permute-start | bytes 196616 | tf_op jit(solution)/shard_map/ppermute | solution.py:25
  35.3 5.9 %collective-permute-start.6 = (f32[32,1,512]{2,1,0:T(1,128)S(1)}, f32[32,1,512]{2,1,0:T(1,128)S(1)}, u32[]{:S(2)}, u32[]{:S(2)}) collective-permute-start(f32[32,1,512]{2,1,0:T(1,128)S(1)} %slice.133), channel_id=1, source_target_pairs={{1,0},{2,1},{3,2},{4,3},{5,4},{6,5},{7,6},{8,7},{9,8},{10,9},{11,1... | collective-permute-start | bytes 196616 | tf_op jit(solution)/shard_map/ppermute | solution.py:25
  44.1 9.5 %copy-start.1 = (f32[32,32,512]{2,1,0:T(8,128)}, f32[32,32,512]{2,1,0:T(8,128)S(1)}, u32[]{:S(2)}) copy-start(f32[32,32,512]{2,1,0:T(8,128)S(1)} %get-tuple-element.37) | copy-start | bytes 6291460
  44.1 9.5 %copy-start.2 = (f32[32,32,512]{2,1,0:T(8,128)}, f32[32,32,512]{2,1,0:T(8,128)S(1)}, u32[]{:S(2)}) copy-start(f32[32,32,512]{2,1,0:T(8,128)S(1)} %get-tuple-element.34) | copy-start | bytes 6291460
  44.1 9.5 %copy-start.3 = (f32[32,32,512]{2,1,0:T(8,128)}, f32[32,32,512]{2,1,0:T(8,128)S(1)}, u32[]{:S(2)}) copy-start(f32[32,32,512]{2,1,0:T(8,128)S(1)} %get-tuple-element.30) | copy-start | bytes 6291460
  44.2 14.6 %collective-permute-start.7 = (f32[32,1,512]{2,1,0:T(1,128)S(1)}, f32[32,1,512]{2,1,0:T(1,128)S(1)}, u32[]{:S(2)}, u32[]{:S(2)}) collective-permute-start(f32[32,1,512]{2,1,0:T(1,128)S(1)} %slice.135), channel_id=1, source_target_pairs={{0,1},{1,2},{2,3},{3,4},{4,5},{5,6},{6,7},{7,8},{8,9},{9,10},{10,1... | collective-permute-start | bytes 196616 | tf_op jit(solution)/shard_map/ppermute | solution.py:25
  46.6 12.2 %collective-permute-start.5 = (f32[1,32,512]{2,1,0:T(8,128)S(1)}, f32[1,32,512]{2,1,0:T(8,128)S(1)}, u32[]{:S(2)}, u32[]{:S(2)}) collective-permute-start(f32[1,32,512]{2,1,0:T(8,128)S(1)} %slice.129), channel_id=1, source_target_pairs={{0,32},{32,64},{64,96},{96,128},{128,160},{160,192},{192,224},{1,3... | collective-permute-start | bytes 196616 | tf_op jit(solution)/shard_map/ppermute | solution.py:25
where the time goes:
time: 119 us; the launch traced here: 118 us
  blocking collectives  48.2 us (41%)
  other arithmetic  34.7 us (29%)
  starting transfers between devices  23.4 us (20%)
  between operations  4.58 us (4%)
  local copies, waits for them, and re-layouts  3.87 us (3%)
  waiting for transfers between devices  3.63 us (3%)
    psum x4, blocking collectives, over_axes(): return functools.reduce(lax.psum, axes, shard)  48.2 us
    ppermute x8, starting transfers between devices, passed_along(): lax.ppermute(value, axis, [(source, source + steps) for source in range(f...  23.4 us
    reduce_sum x1, other arithmetic, per_device(): primal_sum = jnp.sum((updated - primal) ** 2)  8.09 us
    min x1, other arithmetic, per_device(): fresh_i = jnp.clip(dual_i + SIGMA * grad_i, -bound, bound)  4.53 us
    sub x2, other arithmetic, per_device(): smooth[:, 1:] - smooth[:, :-1]  4.41 us
    ppermute x8, waiting for transfers between devices, passed_along(): lax.ppermute(value, axis, [(source, source + steps) for source in range(f...  3.63 us
    sub x1, other arithmetic, per_device(): smooth = 2.0 * updated - primal  3.47 us
    another operation x1, other arithmetic, per_device(): return (primal, jnp.stack([dual_i, dual_x, dual_z]), norms)  3.42 us
  transfers between devices with their start and end apart: 8, of which 3 were waited for; matrix products, arithmetic and copies ran while one was open for 12% of the time, Pallas kernels for 0%

commit v1 on v0

v1 whole, which is shorter than its diff:
```python
import jax
import jax.numpy as jnp
from jax import lax
from jax.experimental import pallas as pl
from jax.experimental.pallas import tpu as pltpu
from jax.sharding import PartitionSpec as P

SIGMA = 0.28
TAU = 0.28
C = TAU / (1.0 + TAU)
C_OLD = C / (1.0 + TAU)
TWO_CS = 2.0 * C * SIGMA

LANES = 128
ROWS = 56
OWN = 8
HALO = 40
AXES = ("inl", "xln")
F32 = jnp.float32


def sent_along(value, axis, steps):
    count = lax.axis_size(axis)
    first, last = (max(0, -steps), min(count, count - steps))
    return lax.ppermute(value, axis, [(s, s + steps) for s in range(first, last)])


def clip(value, bound):
    return jnp.minimum(jnp.maximum(value, -bound), bound)


def last_lane():
    return lax.broadcasted_iota(jnp.int32, (8, LANES), 1) == LANES - 1


def first_lane():
    return lax.broadcasted_iota(jnp.int32, (8, LANES), 1) == 0


def depth_next(tiles):
    rolled = [pltpu.roll(t, LANES - 1, 1) for t in tiles] + [tiles[-1]]
    mask = last_lane()
    return [jnp.where(mask, rolled[j + 1], rolled[j]) for j in range(len(tiles))]


def depth_back(tiles):
    rolled = [jnp.zeros((8, LANES), F32)] + [pltpu.roll(t, 1, 1) for t in tiles]
    mask = first_lane()
    return [jnp.where(mask, rolled[j], rolled[j + 1]) for j in range(len(tiles))]


def pack_kernel(n_hbm, b_hbm, f_ref, g_ref, low, high, sems):
    copies = []
    for k, src in enumerate((n_hbm, b_hbm)):
        copies.append(pltpu.make_async_copy(src.at[:, pl.ds(24, 8), :], high.at[k], sems.at[k, 0]))
        copies.append(pltpu.make_async_copy(src.at[:, pl.ds(0, 8), :], low.at[k], sems.at[k, 1]))
    for c in copies:
        c.start()
    for c in copies:
        c.wait()
    depth = n_hbm.shape[2] // LANES

    def body(i, _):
        for k in range(2):
            for j in range(depth):
                lanes = pl.ds(j * LANES, LANES)
                f_ref[i, j, 2 * k : 2 * k + 2, :] = high[k, i, 6:8, lanes]
                g_ref[i, j, 2 * k : 2 * k + 2, :] = low[k, i, 0:2, lanes]
        return 0

    lax.fori_loop(0, n_hbm.shape[0], body, 0)


def pack(noisy, bound):
    ni, _, nz = noisy.shape
    depth = nz // LANES
    message = jax.ShapeDtypeStruct((ni, depth, 4, LANES), F32)
    return pl.pallas_call(
        pack_kernel,
        out_shape=(message, message),
        in_specs=[pl.BlockSpec(memory_space=pl.ANY)] * 2,
        out_specs=[pl.BlockSpec(memory_space=pltpu.VMEM)] * 2,
        scratch_shapes=[
            pltpu.VMEM((2, ni, 8, nz), F32),
            pltpu.VMEM((2, ni, 8, nz), F32),
            pltpu.SemaphoreType.DMA((2, 2)),
        ],
        compiler_params=pltpu.CompilerParams(vmem_limit_bytes=16 << 20),
        name="pack_faces",
    )(noisy, bound)


def fill_columns(p, i, depth, more, f_ref, g_ref, ne, be):
    for j in range(depth):
        ne[p, j, HALO + 6 : HALO + 8, :] = f_ref[i, j, 0:2, :]
        be[p, j, HALO + 6 : HALO + 8, :] = f_ref[i, j, 2:4, :]
        edge = ne[p, j, HALO - 1 : HALO, :]
        ne[p, j, HALO : HALO + 2, :] = g_ref[i, j, 0:2, :]
        be[p, j, HALO : HALO + 2, :] = g_ref[i, j, 2:4, :]
        ne[p, j, HALO : HALO + 1, :] = jnp.where(more, g_ref[i, j, 0:1, :], edge)


def strip(s):
    return pl.ds(OWN + 8 * s, 8)


def strip_next(s):
    return pl.ds(OWN + 8 * s + 1, 8)


def strip_back(s):
    return pl.ds(OWN + 8 * s - 1, 8)


def scale(p, depth, ne, ve, count=5):
    for j in range(depth):
        for s in range(count):
            ve[p, j, strip(s), :] = SIGMA * ne[p, j, strip(s), :]
        ve[p, j, pl.ds(HALO + 8, 1), :] = ve[p, j, pl.ds(OWN, 1), :]


def first_x(p, depth, ve, be, dx, count=5):
    for j in range(depth):
        for s in reversed(range(count)):
            dx[p, j, strip(s), :] = clip(
                ve[p, j, strip_next(s), :] - ve[p, j, strip(s), :], be[p, j, strip(s), :]
            )
        dx[p, j, pl.ds(OWN - 1, 1), :] = dx[p, j, pl.ds(HALO + 7, 1), :]


def cross_divergence(p, s, depth, ve, be, dx):
    v = [ve[p, j, strip(s), :] for j in range(depth)]
    b = [be[p, j, strip(s), :] for j in range(depth)]
    x = [dx[p, j, strip(s), :] for j in range(depth)]
    z = [clip(n - o, k) for n, o, k in zip(depth_next(v), v, b)]
    back = depth_back(z)
    div = [x[j] - dx[p, j, strip_back(s), :] + (z[j] - back[j]) for j in range(depth)]
    return v, b, x, z, div


def planes_kernel(flags, n_hbm, b_hbm, f_ref, g_ref, up_ref, down_ref, ne, be, ve, dx, sems):
    ni, depth = n_hbm.shape[0], n_hbm.shape[2] // LANES
    more_x = flags[1] > 0
    planes = (0, 1, ni - 2, ni - 1)
    copies = []
    for q, i in enumerate(planes):
        for k, (src, dst) in enumerate(((n_hbm, ne), (b_hbm, be))):
            for j in range(depth):
                copies.append(
                    pltpu.make_async_copy(
                        src.at[i, :, pl.ds(j * LANES, LANES)],
                        dst.at[q, j, pl.ds(OWN, 32), :],
                        sems.at[k, q, j],
                    )
                )
    for c in copies:
        c.start()
    for c in copies:
        c.wait()
    for q, i in enumerate(planes):
        fill_columns(q, i, depth, more_x, f_ref, g_ref, ne, be)
        scale(q, depth, ne, ve)
    for q in (0, 3):
        first_x(q, depth, ve, be, dx)
    for s in range(5):
        for j in range(depth):
            rows = pl.ds(8 * s, 8)
            up_ref[j, rows, :] = ne[3, j, strip(s), :]
            up_ref[j, pl.ds(40 + 8 * s, 8), :] = be[3, j, strip(s), :]
            down_ref[j, rows, :] = ne[0, j, strip(s), :]
    for s in range(4):
        div = cross_divergence(3, s, depth, ve, be, dx)[-1]
        for j in range(depth):
            before = clip(ve[3, j, strip(s), :] - ve[2, j, strip(s), :], be[2, j, strip(s), :])
            up_ref[j, pl.ds(80 + 8 * s, 8), :] = div[j] - before
        div = cross_divergence(0, s, depth, ve, be, dx)[-1]
        for j in range(depth):
            own = clip(ve[1, j, strip(s), :] - ve[0, j, strip(s), :], be[0, j, strip(s), :])
            down_ref[j, pl.ds(40 + 8 * s, 8), :] = div[j] + own


def planes(flags, noisy, bound, from_prev, from_next):
    depth = noisy.shape[2] // LANES
    buffer = pltpu.VMEM((4, depth, ROWS, LANES), F32)
    return pl.pallas_call(
        planes_kernel,
        out_shape=(
            jax.ShapeDtypeStruct((depth, 112, LANES), F32),
            jax.ShapeDtypeStruct((depth, 72, LANES), F32),
        ),
        in_specs=[pl.BlockSpec(memory_space=pltpu.SMEM)]
        + [pl.BlockSpec(memory_space=pl.ANY)] * 2
        + [pl.BlockSpec(memory_space=pltpu.VMEM)] * 2,
        out_specs=[pl.BlockSpec(memory_space=pltpu.VMEM)] * 2,
        scratch_shapes=[buffer] * 4 + [pltpu.SemaphoreType.DMA((2, 4, depth))],
        compiler_params=pltpu.CompilerParams(vmem_limit_bytes=16 << 20),
        name="pack_planes",
    )(flags, noisy, bound, from_prev, from_next)


CHUNK = 8


def main_kernel(
    flags, n_hbm, b_hbm, f_ref, g_ref, up_ref, down_ref,
    u_hbm, d_hbm, sums_ref,
    ne, be, ve, ue, di, dx, dz, dx2, di2, div1, uo, do, in_sems, u_sems, d_sems,
):
    ni, depth = n_hbm.shape[0], n_hbm.shape[2] // LANES
    more_i, more_x = flags[0] > 0, flags[1] > 0
    chunks = ni // CHUNK

    def reads(c):
        return [
            pltpu.make_async_copy(
                src.at[pl.ds(c * CHUNK, CHUNK), :, pl.ds(j * LANES, LANES)],
                dst.at[pl.ds(c * CHUNK + 1, CHUNK), j, pl.ds(OWN, 32), :],
                in_sems.at[k, j, c],
            )
            for k, (src, dst) in enumerate(((n_hbm, ne), (b_hbm, be)))
            for j in range(depth)
        ]

    def writes(c):
        span = pl.ds(c * CHUNK, CHUNK)
        return [pltpu.make_async_copy(uo.at[span], u_hbm.at[span], u_sems.at[c])] + [
            pltpu.make_async_copy(do.at[k, span], d_hbm.at[k, span], d_sems.at[k, c])
            for k in range(3)
        ]

    for c in range(chunks):
        for copy in reads(c):
            copy.start()

    for j in range(depth):
        for s in range(5):
            ne[0, j, strip(s), :] = up_ref[j, pl.ds(8 * s, 8), :]
            be[0, j, strip(s), :] = up_ref[j, pl.ds(40 + 8 * s, 8), :]
    scale(0, depth, ne, ve)

    for copy in reads(0):
        copy.wait()
    fill_columns(1, 0, depth, more_x, f_ref, g_ref, ne, be)
    scale(1, depth, ne, ve)

    for j in range(depth):
        for s in range(5):
            low = clip(ve[1, j, strip(s), :] - ve[0, j, strip(s), :], be[0, j, strip(s), :])
            di[0, j, strip(s), :] = low
            if s < 4:
                part = up_ref[j, pl.ds(80 + 8 * s, 8), :]
                ue[0, j, strip(s), :] = ve[0, j, strip(s), :] + TWO_CS * (part + low)

    def first(p, sums):
        p1, d1 = sums
        first_x(p, depth, ve, be, dx)
        for s in range(5):
            v, b, x, z, div = cross_divergence(p, s, depth, ve, be, dx)
            for j in range(depth):
                i_new = clip(ve[p + 1, j, strip(s), :] - v[j], b[j])
                di[p, j, strip(s), :] = i_new
                total = div[j] + (i_new - di[p - 1, j, strip(s), :])
                ue[p, j, strip(s), :] = v[j] + TWO_CS * total
                if s < 4:
                    dz[p, j, strip(s), :] = z[j]
                    div1[p, j, strip(s), :] = total
                    p1 = p1 + total * total
                    d1 = d1 + (x[j] * x[j] + (i_new * i_new + z[j] * z[j]))
        for j in range(depth):
            edge = ue[p, j, pl.ds(HALO - 1, 1), :]
            ue[p, j, pl.ds(HALO, 1), :] = jnp.where(more_x, ue[p, j, pl.ds(HALO, 1), :], edge)
            ue[p, j, pl.ds(HALO + 8, 1), :] = ue[p, j, pl.ds(OWN, 1), :]
        return p1, d1

    def second_i(p, s, j):
        low = clip(
            di[p, j, strip(s), :] + (ue[p + 1, j, strip(s), :] - ue[p, j, strip(s), :]),
            be[p, j, strip(s), :],
        )
        di2[p, j, strip(s), :] = low
        return low

    def second(p, sums):
        p2, d2 = sums
        i = p - 1
        for j in range(depth):
            for s in (4, 3, 2, 1, 0):
                dx2[p, j, strip(s), :] = clip(
                    dx[p, j, strip(s), :]
                    + (ue[p, j, strip_next(s), :] - ue[p, j, strip(s), :]),
                    be[p, j, strip(s), :],
                )
            dx2[p, j, pl.ds(OWN - 1, 1), :] = dx2[p, j, pl.ds(HALO + 7, 1), :]
        for s in range(4):
            u = [ue[p, j, strip(s), :] for j in range(depth)]
            z_old = [dz[p, j, strip(s), :] for j in range(depth)]
            z_new = [
                clip(o + (n - w), be[p, j, strip(s), :])
                for j, (o, n, w) in enumerate(zip(z_old, depth_next(u), u))
            ]
            back = depth_back(z_new)
            rows = pl.ds(8 * s, 8)
            for j in range(depth):
                lanes = pl.ds(j * LANES, LANES)
                i_new = second_i(p, s, j)
                x_new = dx2[p, j, strip(s), :]
                total = (
                    (x_new - dx2[p, j, strip_back(s), :])
                    + (z_new[j] - back[j])
                    + (i_new - di2[p - 1, j, strip(s), :])
                )
                old = div1[p, j, strip(s), :]
                uo[i, rows, lanes] = ne[p, j, strip(s), :] + (C * total + C_OLD * old)
                do[0, i, rows, lanes] = i_new
                do[1, i, rows, lanes] = x_new
                do[2, i, rows, lanes] = z_new[j]
                gap = total - C * old
                p2 = p2 + gap * gap
                gi = i_new - di[p, j, strip(s), :]
                gx = x_new - dx[p, j, strip(s), :]
                gz = z_new[j] - z_old[j]
                d2 = d2 + (gi * gi + (gx * gx + gz * gz))
        return p2, d2

    zero = jnp.zeros((8, LANES), F32)

    def upper(p):
        @pl.when(p < ni)
        def _():
            @pl.when(p % CHUNK == 0)
            def _():
                for copy in reads(p // CHUNK):
                    copy.wait()

            fill_columns(p + 1, p, depth, more_x, f_ref, g_ref, ne, be)

        @pl.when(p == ni)
        def _():
            for j in range(depth):
                for s in range(5):
                    ne[ni + 1, j, strip(s), :] = jnp.where(
                        more_i, down_ref[j, pl.ds(8 * s, 8), :], ne[ni, j, strip(s), :]
                    )

        scale(p + 1, depth, ne, ve)

    upper(1)
    first_sums = first(1, (zero, zero))
    for s in range(4):
        for j in range(depth):
            second_i(0, s, j)

    def body(p, carry):
        a, b = carry
        upper(p)
        a = first(p, a)
        b = second(p - 1, b)

        @pl.when((p - 1) % CHUNK == 0)
        def _():
            for copy in writes((p - 1) // CHUNK - 1):
                copy.start()

        return a, b

    first_sums, second_sums = lax.fori_loop(
        2, ni + 1, body, (first_sums, (zero, zero))
    )
    for j in range(depth):
        for s in range(4):
            part = down_ref[j, pl.ds(40 + 8 * s, 8), :]
            top = ve[ni + 1, j, strip(s), :] + TWO_CS * (part - di[ni, j, strip(s), :])
            ue[ni + 1, j, strip(s), :] = jnp.where(more_i, top, ue[ni, j, strip(s), :])
    second_sums = second(ni, second_sums)
    for copy in writes(chunks - 1):
        copy.start()
    sums = first_sums + second_sums
    factors = (C * C, 1.0, C * C, 1.0)
    lane = lax.broadcasted_iota(jnp.int32, (1, LANES), 1)
    row = jnp.zeros((1, LANES), F32)
    for k in range(4):
        row = jnp.where(lane == k, factors[k] * jnp.sum(sums[k]), row)
    sums_ref[...] = row
    for c in range(chunks):
        for copy in writes(c):
            copy.wait()


def iterate(flags, noisy, bound, from_prev, from_next, from_below, from_above):
    ni, nx, nz = noisy.shape
    depth = nz // LANES
    buffer = pltpu.VMEM((ni + 2, depth, ROWS, LANES), F32)
    chunks = ni // CHUNK
    return pl.pallas_call(
        main_kernel,
        out_shape=(
            jax.ShapeDtypeStruct((ni, nx, nz), F32),
            jax.ShapeDtypeStruct((3, ni, nx, nz), F32),
            jax.ShapeDtypeStruct((1, LANES), F32),
        ),
        in_specs=[pl.BlockSpec(memory_space=pltpu.SMEM)]
        + [pl.BlockSpec(memory_space=pl.ANY)] * 2
        + [pl.BlockSpec(memory_space=pltpu.VMEM)] * 4,
        out_specs=[pl.BlockSpec(memory_space=pl.ANY)] * 2
        + [pl.BlockSpec(memory_space=pltpu.VMEM)],
        scratch_shapes=[buffer] * 10
        + [
            pltpu.VMEM((ni, nx, nz), F32),
            pltpu.VMEM((3, ni, nx, nz), F32),
            pltpu.SemaphoreType.DMA((2, depth, chunks)),
            pltpu.SemaphoreType.DMA((chunks,)),
            pltpu.SemaphoreType.DMA((3, chunks)),
        ],
        compiler_params=pltpu.CompilerParams(vmem_limit_bytes=58 << 20),
        name="iterate",
    )(flags, noisy, bound, from_prev, from_next, from_below, from_above)


def per_device(noisy, bound):
    count_i, count_x = lax.axis_size("inl"), lax.axis_size("xln")
    flags = jnp.stack(
        [
            (lax.axis_index("inl") < count_i - 1).astype(jnp.int32),
            (lax.axis_index("xln") < count_x - 1).astype(jnp.int32),
        ]
    )
    to_next, to_prev = pack(noisy, bound)
    from_prev = sent_along(to_next, "xln", 1)
    from_next = sent_along(to_prev, "xln", -1)
    up, down = planes(flags, noisy, bound, from_prev, from_next)
    from_below = sent_along(up, "inl", 1)
    from_above = sent_along(down, "inl", -1)
    primal, dual, sums = iterate(
        flags, noisy, bound, from_prev, from_next, from_below, from_above
    )
    devices = count_i * count_x
    spread = jnp.broadcast_to(sums[:, :4], (devices, 4))
    parts = lax.all_to_all(spread, AXES, 0, 0, tiled=True)
    norms = jnp.sqrt(jnp.sum(parts, axis=0)).reshape(2, 2)
    return primal, dual, norms


def solution(mesh):
    in_specs = (P("inl", "xln", None), P("inl", "xln", None))
    out_specs = (P("inl", "xln", None), P(None, "inl", "xln", None), P())
    return jax.shard_map(
        per_device, mesh=mesh, in_specs=in_specs, out_specs=out_specs, check_vma=False
    )
```

time: 119 us -> 77.9 us (0.65)
  other arithmetic: 34.7 us -> 0.36 us
  blocking collectives: 48.2 us -> 28.3 us
  Pallas kernels: 0 us -> 18.8 us
  starting transfers between devices: 23.4 us -> 11.4 us
  waiting for transfers between devices: 3.63 us -> 10.4 us
  between operations: 4.58 us -> 0.74 us
  local copies, waits for them, and re-layouts: 3.87 us -> 7.52 us
    psum x4 -> x0, blocking collectives: 48.2 us -> none  [over_axes(): return functools.reduce(lax.psum, axes, shard)]
    all_to_all x0 -> x1, blocking collectives: none -> 28.3 us  [per_device(): parts = lax.all_to_all(spread, AXES, 0, 0, tiled=True)]
    pallas_call x0 -> x3, Pallas kernels: none -> 18.8 us  [the longest x1 17 us: iterate(): pl.pallas_call(main_kernel, out_shape=(jax.ShapeDtypeStruct((ni, nx, nz),...]
    sub x7 -> x0, other arithmetic: 12.4 us -> none  [the longest x2 4.41 us: per_device(): smooth[:, 1:] - smooth[:, :-1]]
    ppermute x8 -> x4, starting transfers between devices: 23.4 us -> 11.4 us  [sent_along(): lax.ppermute(value, axis, [(s, s + steps) for s in range(first, last)])]
    reduce_sum x2 -> x1, other arithmetic: 11 us -> 0.29 us  [per_device(): norms = jnp.sqrt(jnp.sum(parts, axis=0)).reshape(2, 2)]
    ppermute x8 -> x4, waiting for transfers between devices: 3.63 us -> 10.4 us  [sent_along(): lax.ppermute(value, axis, [(s, s + steps) for s in range(first, last)])]
    unnamed x10 -> x18, local copies, waits for them, and re-layouts: 0.02 us -> 6.13 us
  transfers between devices with their start and end apart: 8 -> 4, of which waited for: 3 -> 3; matrix products, arithmetic and copies ran while one was open for 12% -> 0% of each run, Pallas kernels for 0% -> 0%
where the time goes in v1:
time: 77.9 us; the launch traced here: 77.5 us
  blocking collectives  28.3 us (36%)
  Pallas kernels  18.8 us (24%)
  starting transfers between devices  11.4 us (15%)
  waiting for transfers between devices  10.4 us (13%)
  local copies, waits for them, and re-layouts  7.52 us (10%)
    all_to_all x1, blocking collectives, per_device(): parts = lax.all_to_all(spread, AXES, 0, 0, tiled=True)  28.3 us
    pallas_call x1, Pallas kernels, iterate(): pl.pallas_call(main_kernel, out_shape=(jax.ShapeDtypeStruct((ni, nx, nz),...  17 us
    ppermute x4, starting transfers between devices, sent_along(): lax.ppermute(value, axis, [(s, s + steps) for s in range(first, last)])  11.4 us
    ppermute x4, waiting for transfers between devices, sent_along(): lax.ppermute(value, axis, [(s, s + steps) for s in range(first, last)])  10.4 us
    unnamed x18, local copies, waits for them, and re-layouts  6.13 us
  transfers between devices with their start and end apart: 4, of which 3 were waited for; matrix products, arithmetic and copies ran while one was open for 0% of the time, Pallas kernels for 0%

profile of v1, /device:TPU:1, one launch (start us, length us, event | category | flops | bytes accessed | tf_op | source)
XLA Modules:
  0.0 77.5 jit_solution(14398759145384538753)
XLA Ops:
  0.6 0.0 copy-start
  0.6 1.6 %copy-done = f32[32,32,512]{2,1,0:T(8,128)S(1)} copy-done((f32[32,32,512]{2,1,0:T(8,128)S(1)}, f32[32,32,512]{2,1,0:T(8,128)}, u32[]{:S(2)}) %copy-start) | copy-done | bytes 2097176
  2.2 1.6 %copy-done.2 = f32[32,32,512]{2,1,0:T(8,128)S(1)} copy-done((f32[32,32,512]{2,1,0:T(8,128)S(1)}, f32[32,32,512]{2,1,0:T(8,128)}, u32[]{:S(2)}) %copy-start.2) | copy-done | bytes 2097176
  3.8 0.5 pack_faces.1
  4.4 4.6 %collective-permute-start = (f32[32,4,4,128]{3,2,1,0:T(4,128)S(1)}, f32[32,4,4,128]{3,2,1,0:T(4,128)S(1)}, u32[]{:S(2)}, u32[]{:S(2)}) collective-permute-start(f32[32,4,4,128]{3,2,1,0:T(4,128)S(1)} %get-tuple-element.10), channel_id=1, source_target_pairs={{0,1},{1,2},{2,3},{3,4},{4,5},{5,6},{6,7},{7,8},{8,9},{9,10},{10,1... | collective-permute-start | bytes 786440 | tf_op jit(solution)/shard_map/ppermute | solution.py:25
  9.0 1.9 %collective-permute-start.1 = (f32[32,4,4,128]{3,2,1,0:T(4,128)S(1)}, f32[32,4,4,128]{3,2,1,0:T(4,128)S(1)}, u32[]{:S(2)}, u32[]{:S(2)}) collective-permute-start(f32[32,4,4,128]{3,2,1,0:T(4,128)S(1)} %get-tuple-element.11), channel_id=1, source_target_pairs={{1,0},{2,1},{3,2},{4,3},{5,4},{6,5},{7,6},{8,7},{9,8},{10,9},{11,1... | collective-permute-start | bytes 786440 | tf_op jit(solution)/shard_map/ppermute | solution.py:25
  10.9 0.1 add_convert_fusion.flags
  11.0 1.3 %collective-permute-done.f_ref = f32[32,4,4,128]{3,2,1,0:T(4,128)S(1)} collective-permute-done((f32[32,4,4,128]{3,2,1,0:T(4,128)S(1)}, f32[32,4,4,128]{3,2,1,0:T(4,128)S(1)}, u32[]{:S(2)}, u32[]{:S(2)}) %collective-permute-start) | collective-permute-done | bytes 262176 | tf_op jit(solution)/shard_map/ppermute | solution.py:25
  12.3 4.4 %collective-permute-done.1.g_ref = f32[32,4,4,128]{3,2,1,0:T(4,128)S(1)} collective-permute-done((f32[32,4,4,128]{3,2,1,0:T(4,128)S(1)}, f32[32,4,4,128]{3,2,1,0:T(4,128)S(1)}, u32[]{:S(2)}, u32[]{:S(2)}) %collective-permute-start.1) | collective-permute-done | bytes 262176 | tf_op jit(solution)/shard_map/ppermute | solution.py:25
  16.7 0.0 copy-done.1
  16.7 1.6 %copy-done.3 = f32[32,32,512]{2,1,0:T(8,128)S(1)} copy-done((f32[32,32,512]{2,1,0:T(8,128)S(1)}, f32[32,32,512]{2,1,0:T(8,128)}, u32[]{:S(2)}) %copy-start.3) | copy-done | bytes 2097176
  18.3 1.2 %pack_planes.1 = (f32[4,112,128]{2,1,0:T(8,128)S(1)}, f32[4,72,128]{2,1,0:T(8,128)S(1)}) custom-call(s32[2]{0:T(128)S(1)} %add_convert_fusion.flags, f32[32,32,512]{2,1,0:T(8,128)S(1)} %copy-done.1, f32[32,32,512]{2,1,0:T(8,128)S(1)} %copy-done.3, f32[32,4,4,128]{3,2,1,0:T(4,128)S(1)} %collective-permute-done.f_ref, ...), custom_call_target="tpu_custom_call" | custom-call | tf_op jit(solution)/shard_map/pack_planes/pallas_call | solution.py:185
  19.6 3.6 %collective-permute-start.2 = (f32[4,112,128]{2,1,0:T(8,128)S(1)}, f32[4,112,128]{2,1,0:T(8,128)S(1)}, u32[]{:S(2)}, u32[]{:S(2)}) collective-permute-start(f32[4,112,128]{2,1,0:T(8,128)S(1)} %get-tuple-element.12), channel_id=1, source_target_pairs={{0,32},{32,64},{64,96},{96,128},{128,160},{160,192},{192,224},{1,3... | collective-permute-start | bytes 688136 | tf_op jit(solution)/shard_map/ppermute | solution.py:25
  23.1 1.3 %collective-permute-start.3 = (f32[4,72,128]{2,1,0:T(8,128)S(1)}, f32[4,72,128]{2,1,0:T(8,128)S(1)}, u32[]{:S(2)}, u32[]{:S(2)}) collective-permute-start(f32[4,72,128]{2,1,0:T(8,128)S(1)} %get-tuple-element.13), channel_id=1, source_target_pairs={{32,0},{64,32},{96,64},{128,96},{160,128},{192,160},{224,192},{33,... | collective-permute-start | bytes 442376 | tf_op jit(solution)/shard_map/ppermute | solution.py:25
  24.4 4.8 %collective-permute-done.3.down_ref = f32[4,72,128]{2,1,0:T(8,128)S(1)} collective-permute-done((f32[4,72,128]{2,1,0:T(8,128)S(1)}, f32[4,72,128]{2,1,0:T(8,128)S(1)}, u32[]{:S(2)}, u32[]{:S(2)}) %collective-permute-start.3) | collective-permute-done | bytes 147488 | tf_op jit(solution)/shard_map/ppermute | solution.py:25
  29.2 0.0 collective-permute-done.2.up_ref
  29.2 0.7 copy-done.8
  29.9 0.7 copy-done.7
  30.5 17.0 %iterate.1 = (f32[32,32,512]{2,1,0:T(8,128)}, f32[3,32,32,512]{3,2,1,0:T(8,128)}, f32[1,128]{1,0:T(1,128)}) custom-call(s32[2]{0:T(128)} %copy-done.6, f32[32,32,512]{2,1,0:T(8,128)} %n_hbm.5, f32[32,32,512]{2,1,0:T(8,128)} %b_hbm.5, f32[32,4,4,128]{3,2,1,0:T(4,128)} %copy-done.4, f32[32,4,4,128]{3,2,1,0:T(4,128)} %copy-done.5, f32[4,112,128]{2,1,0:T(8,128)} %copy-done.7, ...), custom_call_target="tpu_custom_call" | custom-call | tf_op jit(solution)/shard_map/iterate/pallas_call | solution.py:394
  47.5 0.7 slice_bitcast_fusion
  48.2 0.1 broadcast_in_dim.2
  48.3 28.3 %all_to_all.6 = f32[256,1,4]{2,1,0:T(1,128)S(1)} all-to-all(f32[256,1,4]{2,1,0:T(1,128)S(1)} %broadcast_in_dim.2), channel_id=1, replica_groups=mesh['inl'=8,'xln'=32] {'inl','xln'}, dimensions={0} | all-to-all | bytes 8192 | tf_op jit(solution)/shard_map/all_to_all | solution.py:438
  76.6 0.3 reduce_sum.9
  76.9 0.7 sqrt.8
  (12 shorter events, 0.0 us)
Async XLA Ops:
  0.6 1.6 %copy-start = (f32[32,32,512]{2,1,0:T(8,128)S(1)}, f32[32,32,512]{2,1,0:T(8,128)}, u32[]{:S(2)}) copy-start(f32[32,32,512]{2,1,0:T(8,128)} %n_hbm.5) | copy-start | bytes 6291460
  2.2 1.6 %copy-start.2 = (f32[32,32,512]{2,1,0:T(8,128)S(1)}, f32[32,32,512]{2,1,0:T(8,128)}, u32[]{:S(2)}) copy-start(f32[32,32,512]{2,1,0:T(8,128)} %b_hbm.5) | copy-start | bytes 6291460
  3.8 12.9 %copy-start.1 = (f32[32,32,512]{2,1,0:T(8,128)S(1)}, f32[32,32,512]{2,1,0:T(8,128)}, u32[]{:S(2)}) copy-start(f32[32,32,512]{2,1,0:T(8,128)} %n_hbm.5) | copy-start | bytes 6291460
  4.4 7.9 %collective-permute-start = (f32[32,4,4,128]{3,2,1,0:T(4,128)S(1)}, f32[32,4,4,128]{3,2,1,0:T(4,128)S(1)}, u32[]{:S(2)}, u32[]{:S(2)}) collective-permute-start(f32[32,4,4,128]{3,2,1,0:T(4,128)S(1)} %get-tuple-element.10), channel_id=1, source_target_pairs={{0,1},{1,2},{2,3},{3,4},{4,5},{5,6},{6,7},{7,8},{8,9},{9,10},{10,1... | collective-permute-start | bytes 786440 | tf_op jit(solution)/shard_map/ppermute | solution.py:25
  9.0 7.7 %collective-permute-start.1 = (f32[32,4,4,128]{3,2,1,0:T(4,128)S(1)}, f32[32,4,4,128]{3,2,1,0:T(4,128)S(1)}, u32[]{:S(2)}, u32[]{:S(2)}) collective-permute-start(f32[32,4,4,128]{3,2,1,0:T(4,128)S(1)} %get-tuple-element.11), channel_id=1, source_target_pairs={{1,0},{2,1},{3,2},{4,3},{5,4},{6,5},{7,6},{8,7},{9,8},{10,9},{11,1... | collective-permute-start | bytes 786440 | tf_op jit(solution)/shard_map/ppermute | solution.py:25
  11.0 8.5 %copy-start.6 = (s32[2]{0:T(128)}, s32[2]{0:T(128)S(1)}, u32[]{:S(2)}) copy-start(s32[2]{0:T(128)S(1)} %add_convert_fusion.flags) | copy-start | bytes 28
  12.3 7.3 %copy-start.4 = (f32[32,4,4,128]{3,2,1,0:T(4,128)}, f32[32,4,4,128]{3,2,1,0:T(4,128)S(1)}, u32[]{:S(2)}) copy-start(f32[32,4,4,128]{3,2,1,0:T(4,128)S(1)} %collective-permute-done.f_ref) | copy-start | bytes 786436
  16.7 1.6 %copy-start.3 = (f32[32,32,512]{2,1,0:T(8,128)S(1)}, f32[32,32,512]{2,1,0:T(8,128)}, u32[]{:S(2)}) copy-start(f32[32,32,512]{2,1,0:T(8,128)} %b_hbm.5) | copy-start | bytes 6291460
  18.3 1.3 %copy-start.5 = (f32[32,4,4,128]{3,2,1,0:T(4,128)}, f32[32,4,4,128]{3,2,1,0:T(4,128)S(1)}, u32[]{:S(2)}) copy-start(f32[32,4,4,128]{3,2,1,0:T(4,128)S(1)} %collective-permute-done.1.g_ref) | copy-start | bytes 786436
  19.6 9.6 %collective-permute-start.2 = (f32[4,112,128]{2,1,0:T(8,128)S(1)}, f32[4,112,128]{2,1,0:T(8,128)S(1)}, u32[]{:S(2)}, u32[]{:S(2)}) collective-permute-start(f32[4,112,128]{2,1,0:T(8,128)S(1)} %get-tuple-element.12), channel_id=1, source_target_pairs={{0,32},{32,64},{64,96},{96,128},{128,160},{160,192},{192,224},{1,3... | collective-permute-start | bytes 688136 | tf_op jit(solution)/shard_map/ppermute | solution.py:25
  23.1 6.1 %collective-permute-start.3 = (f32[4,72,128]{2,1,0:T(8,128)S(1)}, f32[4,72,128]{2,1,0:T(8,128)S(1)}, u32[]{:S(2)}, u32[]{:S(2)}) collective-permute-start(f32[4,72,128]{2,1,0:T(8,128)S(1)} %get-tuple-element.13), channel_id=1, source_target_pairs={{32,0},{64,32},{96,64},{128,96},{160,128},{192,160},{224,192},{33,... | collective-permute-start | bytes 442376 | tf_op jit(solution)/shard_map/ppermute | solution.py:25
  29.2 0.7 copy-start.8
  29.9 0.7 copy-start.7

commit v2 on v0

v2 whole, which is shorter than its diff:
```python
import jax
import jax.numpy as jnp
from jax import lax
from jax.experimental import pallas as pl
from jax.experimental.pallas import tpu as pltpu
from jax.sharding import PartitionSpec as P

SIGMA = 0.28
TAU = 0.28
C = TAU / (1.0 + TAU)
C_OLD = C / (1.0 + TAU)
TWO_CS = 2.0 * C * SIGMA

LANES = 128
ROWS = 56
OWN = 8
HALO = 40
AXES = ("inl", "xln")
F32 = jnp.float32


def swapped(value, axis, first):
    count = lax.axis_size(axis)
    pairs = []
    for low in range(first, count - 1, 2):
        pairs += [(low, low + 1), (low + 1, low)]
    return lax.ppermute(value, axis, pairs)


def clip(value, bound):
    return jnp.minimum(jnp.maximum(value, -bound), bound)


def last_lane():
    return lax.broadcasted_iota(jnp.int32, (8, LANES), 1) == LANES - 1


def first_lane():
    return lax.broadcasted_iota(jnp.int32, (8, LANES), 1) == 0


def depth_next(tiles):
    rolled = [pltpu.roll(t, LANES - 1, 1) for t in tiles] + [tiles[-1]]
    mask = last_lane()
    return [jnp.where(mask, rolled[j + 1], rolled[j]) for j in range(len(tiles))]


def depth_back(tiles):
    rolled = [jnp.zeros((8, LANES), F32)] + [pltpu.roll(t, 1, 1) for t in tiles]
    mask = first_lane()
    return [jnp.where(mask, rolled[j], rolled[j + 1]) for j in range(len(tiles))]


def pack_kernel(flags, n_hbm, b_hbm, a_ref, c_ref, n4_ref, b4_ref, slab, sems, plane_sems):
    ni, nx, depth = n_hbm.shape[0], n_hbm.shape[1], n_hbm.shape[2] // LANES
    even = flags[3] == 0
    columns, planes = [], []
    for k, src in enumerate((n_hbm, b_hbm)):
        for m, start in enumerate((jnp.where(even, nx - 8, 0), jnp.where(even, 0, nx - 8))):
            start = pl.multiple_of(start, 8)
            columns.append(
                pltpu.make_async_copy(src.at[:, pl.ds(start, 8), :], slab.at[m, k], sems.at[m, k])
            )
    for k, (src, dst) in enumerate(((n_hbm, n4_ref), (b_hbm, b4_ref))):
        for q, i in enumerate((0, ni - 2)):
            planes.append(
                pltpu.make_async_copy(
                    src.at[pl.ds(i, 2)], dst.at[pl.ds(2 * q, 2)], plane_sems.at[k, q]
                )
            )
    for c in columns + planes:
        c.start()
    for c in columns:
        c.wait()

    def body(i, _):
        for k in range(2):
            for j in range(depth):
                lanes = pl.ds(j * LANES, LANES)
                a_ref[i, j, 2 * k : 2 * k + 2, :] = jnp.where(
                    even, slab[0, k, i, 6:8, lanes], slab[0, k, i, 0:2, lanes]
                )
                c_ref[i, j, 2 * k : 2 * k + 2, :] = jnp.where(
                    even, slab[1, k, i, 0:2, lanes], slab[1, k, i, 6:8, lanes]
                )
        return 0

    lax.fori_loop(0, ni, body, 0, unroll=2)
    for c in planes:
        c.wait()


HBM = pltpu.MemorySpace.HBM
VMEM = pltpu.MemorySpace.VMEM


def pack(flags, noisy, bound):
    ni, nx, nz = noisy.shape
    depth = nz // LANES
    message = pltpu.VMEM((ni, depth, 4, LANES), F32)
    boundary = pltpu.VMEM((4, nx, nz), F32)
    return pl.pallas_call(
        pack_kernel,
        out_shape=(message, message, boundary, boundary),
        in_specs=[pl.BlockSpec(memory_space=pltpu.SMEM)] + [pl.BlockSpec(memory_space=HBM)] * 2,
        out_specs=[pl.BlockSpec(memory_space=VMEM)] * 4,
        scratch_shapes=[
            pltpu.VMEM((2, 2, ni, 8, nz), F32),
            pltpu.SemaphoreType.DMA((2, 2)),
            pltpu.SemaphoreType.DMA((2, 2)),
        ],
        compiler_params=pltpu.CompilerParams(vmem_limit_bytes=8 << 20),
        name="pack_faces",
    )(flags, noisy, bound)


def strip(s):
    return pl.ds(OWN + 8 * s, 8)


def strip_next(s):
    return pl.ds(OWN + 8 * s + 1, 8)


def strip_back(s):
    return pl.ds(OWN + 8 * s - 1, 8)


def wrap_rows(field, p, depth):
    for j in range(depth):
        field[p, j, pl.ds(HALO + 8, 1), :] = field[p, j, pl.ds(OWN, 1), :]


def scale(p, depth, image_of, ve):
    for j in range(depth):
        for s in range(5):
            ve[p, j, strip(s), :] = SIGMA * image_of(p, j, s)
    wrap_rows(ve, p, depth)


def tile(field, p, j, s):
    return field[p, pl.ds(8 * s, 8), pl.ds(j * LANES, LANES)]


def x_dual(p, s, depth, ve, v, b, c):
    return [
        clip2(ve[p, j, strip_next(s), :] - v[j], b[j], c[j]) for j in range(depth)
    ]


def clip2(value, bound, below):
    return jnp.minimum(jnp.maximum(value, below), bound)


ORDER = (4, 0, 1, 2, 3)


def crossline(p, q, depth, ve, bound_of, dx, then):
    for s in (3,) + ORDER:
        v = [ve[p, j, strip(s), :] for j in range(depth)]
        b = [bound_of(p, j, s) for j in range(depth)]
        c = [-k for k in b]
        x = x_dual(p, s, depth, ve, v, b, c)
        for j in range(depth):
            dx[q, j, strip(s), :] = x[j]
        if s == 3:
            break
    for s in ORDER:
        v = [ve[p, j, strip(s), :] for j in range(depth)]
        b = [bound_of(p, j, s) for j in range(depth)]
        c = [-k for k in b]
        if s == 3:
            x = [dx[q, j, strip(s), :] for j in range(depth)]
        else:
            x = x_dual(p, s, depth, ve, v, b, c)
            for j in range(depth):
                dx[q, j, strip(s), :] = x[j]
        z = [clip2(n - o, k, m) for n, o, k, m in zip(depth_next(v), v, b, c)]
        back = depth_back(z)
        div = [x[j] - dx[q, j, strip_back(s), :] + (z[j] - back[j]) for j in range(depth)]
        then(s, v, b, c, x, z, div)
        if s == 4:
            for j in range(depth):
                dx[q, j, pl.ds(OWN - 1, 1), :] = dx[q, j, pl.ds(HALO + 7, 1), :]


def planes_kernel(
    flags, n4_ref, b4_ref, sent_a, sent_c, got_a, got_c,
    a_ref, c_ref, hn, hb, ve, dx,
):
    ni, depth = got_a.shape[0], got_a.shape[1]
    more_x, even_x, even_i = flags[1] > 0, flags[3] == 0, flags[2] == 0

    def sort(i, _):
        for j in range(depth):
            last = jnp.where(even_x, sent_a[i, j, 1:2, :], sent_c[i, j, 1:2, :])
            a_n, c_n = got_a[i, j, 0:2, :], got_c[i, j, 0:2, :]
            a_b, c_b = got_a[i, j, 2:4, :], got_c[i, j, 2:4, :]
            hn[i, j, 6:8, :] = jnp.where(even_x, c_n, a_n)
            hb[i, j, 6:8, :] = jnp.where(even_x, c_b, a_b)
            above = jnp.where(even_x, a_n, c_n)
            hn[i, j, 0:2, :] = above
            hb[i, j, 0:2, :] = jnp.where(even_x, a_b, c_b)
            hn[i, j, 0:1, :] = jnp.where(more_x, above[0:1], last)
        return 0

    lax.fori_loop(0, ni, sort, 0, unroll=2)
    place = (0, 1, ni - 2, ni - 1)

    def image_of(q, j, s):
        return hn[place[q], j, 0:8, :] if s == 4 else tile(n4_ref, q, j, s)

    def bound_of(q, j, s):
        return hb[place[q], j, 0:8, :] if s == 4 else tile(b4_ref, q, j, s)

    for q in range(4):
        scale(q, depth, image_of, ve)

    def up(ref):
        for s in range(5):
            for j in range(depth):
                ref[j, pl.ds(8 * s, 8), :] = image_of(3, j, s)
                ref[j, pl.ds(40 + 8 * s, 8), :] = bound_of(3, j, s)

        def then(s, v, b, c, x, z, div):
            if s == 4:
                return
            for j in range(depth):
                before = clip(v[j] - ve[2, j, strip(s), :], bound_of(2, j, s))
                ref[j, pl.ds(80 + 8 * s, 8), :] = div[j] - before

        crossline(3, 3, depth, ve, bound_of, dx, then)

    def down(ref):
        for s in range(5):
            for j in range(depth):
                ref[j, pl.ds(8 * s, 8), :] = image_of(0, j, s)

        def then(s, v, b, c, x, z, div):
            if s == 4:
                return
            for j in range(depth):
                own = clip2(ve[1, j, strip(s), :] - v[j], b[j], c[j])
                ref[j, pl.ds(40 + 8 * s, 8), :] = div[j] + own

        crossline(0, 0, depth, ve, bound_of, dx, then)

    @pl.when(even_i)
    def _():
        up(a_ref)
        down(c_ref)

    @pl.when(jnp.logical_not(even_i))
    def _():
        down(a_ref)
        up(c_ref)


def planes(flags, n4, b4, sent_a, sent_c, got_a, got_c):
    ni, depth = got_a.shape[0], got_a.shape[1]
    buffer = pltpu.VMEM((4, depth, ROWS, LANES), F32)
    return pl.pallas_call(
        planes_kernel,
        out_shape=(pltpu.VMEM((depth, 112, LANES), F32),) * 2
        + (pltpu.VMEM((ni, depth, 8, LANES), F32),) * 2,
        in_specs=[pl.BlockSpec(memory_space=pltpu.SMEM)] + [pl.BlockSpec(memory_space=VMEM)] * 6,
        out_specs=[pl.BlockSpec(memory_space=VMEM)] * 4,
        scratch_shapes=[buffer] * 2,
        compiler_params=pltpu.CompilerParams(vmem_limit_bytes=8 << 20),
        name="pack_planes",
    )(flags, n4, b4, sent_a, sent_c, got_a, got_c)


class Fields:
    def __init__(self, ring, **fields):
        self.ring = ring
        self.__dict__.update(fields)


class Split:
    def __init__(self, given, own, slots):
        self.given, self.own, self.slots = given, own, slots

    def __getitem__(self, index):
        return (self.given if index[0] in self.slots else self.own)[index]

    def __setitem__(self, index, value):
        self.own[index] = value


def first(t, p, depth, more_x, sums):
    sums = list(sums)
    q, before = t.ring(p), t.ring(p - 1)

    def then(s, v, b, c, x, z, div):
        for j in range(depth):
            i_new = clip2(t.ve[p + 1, j, strip(s), :] - v[j], b[j], c[j])
            t.di[q, j, strip(s), :] = i_new
            total = div[j] + (i_new - t.di[before, j, strip(s), :])
            t.ue[p, j, strip(s), :] = v[j] + TWO_CS * total
            if s < 4:
                t.dz[q, j, strip(s), :] = z[j]
                t.div1[q, j, strip(s), :] = total
                sums[0] = sums[0] + total * total
                sums[1] = sums[1] + (x[j] * x[j] + (i_new * i_new + z[j] * z[j]))

    crossline(p, q, depth, t.ve, t.bound_of, t.dx, then)
    for j in range(depth):
        edge = t.ue[p, j, pl.ds(HALO - 1, 1), :]
        t.ue[p, j, pl.ds(HALO, 1), :] = jnp.where(more_x, t.ue[p, j, pl.ds(HALO, 1), :], edge)
    wrap_rows(t.ue, p, depth)
    return tuple(sums)


def second_i(t, p, s, j):
    q = t.ring(p)
    t.di2[q, j, strip(s), :] = clip(
        t.di[q, j, strip(s), :] + (t.ue[p + 1, j, strip(s), :] - t.ue[p, j, strip(s), :]),
        t.bound_of(p, j, s),
    )


def second(t, p, o, depth, sums, uo, do):
    p2, d2 = sums
    q, before = t.ring(p), t.ring(p - 1)
    for s in ORDER:
        u = [t.ue[p, j, strip(s), :] for j in range(depth)]
        b = [t.bound_of(p, j, s) for j in range(depth)]
        c = [-k for k in b]
        x_old = [t.dx[q, j, strip(s), :] for j in range(depth)]
        x_new = [
            clip2(x_old[j] + (t.ue[p, j, strip_next(s), :] - u[j]), b[j], c[j])
            for j in range(depth)
        ]
        for j in range(depth):
            t.dx2[q, j, strip(s), :] = x_new[j]
        if s == 4:
            for j in range(depth):
                t.dx2[q, j, pl.ds(OWN - 1, 1), :] = t.dx2[q, j, pl.ds(HALO + 7, 1), :]
            continue
        z_old = [t.dz[q, j, strip(s), :] for j in range(depth)]
        z_new = [
            clip2(z_old[j] + (n - u[j]), b[j], c[j]) for j, n in enumerate(depth_next(u))
        ]
        back = depth_back(z_new)
        rows = pl.ds(8 * s, 8)
        for j in range(depth):
            lanes = pl.ds(j * LANES, LANES)
            i_old = t.di[q, j, strip(s), :]
            i_new = clip2(i_old + (t.ue[p + 1, j, strip(s), :] - u[j]), b[j], c[j])
            t.di2[q, j, strip(s), :] = i_new
            total = (
                (x_new[j] - t.dx2[q, j, strip_back(s), :])
                + (z_new[j] - back[j])
                + (i_new - t.di2[before, j, strip(s), :])
            )
            old = t.div1[q, j, strip(s), :]
            uo[o, rows, lanes] = t.image_of(p, j, s) + (C * total + C_OLD * old)
            do[0, o, rows, lanes] = i_new
            do[1, o, rows, lanes] = x_new[j]
            do[2, o, rows, lanes] = z_new[j]
            gap = total - C * old
            p2 = p2 + gap * gap
            gi = i_new - i_old
            gx = x_new[j] - x_old[j]
            gz = z_new[j] - z_old[j]
            d2 = d2 + (gi * gi + (gx * gx + gz * gz))
    return p2, d2


KEPT = {1: 0, 2: 1, 5: 2, 6: 3}


def boundary_planes(ni):
    return 0, 1, ni - 2, ni - 1


CHUNK = 4
PART = 2
HANDED = (
    ("ve", (1, 2, 5, 6)),
    ("ue", (2, 3, 4, 5)),
    ("di", (2, 5)),
    ("dx", (2, 5)),
    ("dz", (2, 5)),
    ("div1", (2, 5)),
    ("di2", (4,)),
)


def inner_kernel(flags, n_hbm, b_hbm, hn, hb, u_hbm, d_hbm, sums_ref, *refs):
    handed, refs = refs[: len(HANDED)], refs[len(HANDED) :]
    ne, be, ve, ue, di, dx, dz, div1, dx2, di2, uo, do, in_sems, u_sems, d_sems = refs
    ni, depth = n_hbm.shape[0], n_hbm.shape[2] // LANES
    more_x = flags[1] > 0

    def bound_of(p, j, s):
        return hb[p, j, 0:8, :] if s == 4 else tile(be, p, j, s)

    def image_of(p, j, s):
        return hn[p, j, 0:8, :] if s == 4 else tile(ne, p, j, s)

    t = Fields(
        lambda p: p % 4,
        bound_of=bound_of, image_of=image_of, ve=ve, ue=ue, di=di, dx=dx, dz=dz, div1=div1, dx2=dx2, di2=di2,
    )
    chunks, parts = ni // CHUNK, (ni - 4) // PART

    def reads(c):
        span = pl.ds(c * CHUNK, CHUNK)
        return [
            pltpu.make_async_copy(src.at[span], dst.at[span], in_sems.at[k, c])
            for k, (src, dst) in enumerate(((n_hbm, ne), (b_hbm, be)))
        ]

    def writes(c):
        span = pl.ds(c * PART + 2, PART)
        return [pltpu.make_async_copy(uo.at[span], u_hbm.at[span], u_sems.at[c])] + [
            pltpu.make_async_copy(do.at[k, span], d_hbm.at[k, span], d_sems.at[k, c])
            for k in range(3)
        ]

    def hand(slots):
        for ref, (name, wanted) in zip(handed, HANDED):
            field = getattr(t, name)
            short = name in ("di", "dx", "dz", "div1", "di2")
            for slot in wanted:
                if slot in slots:
                    plane = slot - 1 if slot < 4 else ni - 7 + slot
                    place = plane % 4 if short else plane
                    for j in range(depth):
                        for s in range(5):
                            if s < 4 or name not in ("dz", "div1", "di2"):
                                ref[slot, j, strip(s), :] = field[place, j, strip(s), :]
                        if name in ("ve", "ue"):
                            ref[slot, j, pl.ds(HALO + 8, 1), :] = field[place, j, pl.ds(HALO + 8, 1), :]

    def ready(p):
        scale(p, depth, image_of, ve)

    for c in range(chunks):
        for copy in reads(c):
            copy.start()
    for copy in reads(0):
        copy.wait()
    for p in range(4):
        ready(p)
    for j in range(depth):
        for s in range(5):
            di[0, j, strip(s), :] = clip(
                ve[1, j, strip(s), :] - ve[0, j, strip(s), :], bound_of(0, j, s)
            )
    zero = jnp.zeros((8, LANES), F32)
    a = first(t, 1, depth, more_x, (zero, zero))
    a = first(t, 2, depth, more_x, a)
    for s in range(4):
        for j in range(depth):
            second_i(t, 1, s, j)
    hand((1, 2, 3))

    def body(p, carry):
        a, b = carry

        @pl.when((p + 1) % CHUNK == 0)
        def _():
            for copy in reads((p + 1) // CHUNK):
                copy.wait()

        ready(p + 1)
        a = first(t, p, depth, more_x, a)
        b = second(t, p - 1, p - 1, depth, b, uo, do)

        @pl.when(p % PART == 0)
        def _():
            for copy in writes(p // PART - 2):
                copy.start()

        return a, b

    a, b = lax.fori_loop(3, ni - 1, body, (a, (zero, zero)))
    hand((4, 5, 6))
    for k, total in enumerate(a + b):
        sums_ref[k] = total
    for c in range(parts):
        for copy in writes(c):
            copy.wait()


def inner(flags, noisy, bound, halo_n, halo_b):
    ni, nx, nz = noisy.shape
    depth = nz // LANES
    full = pltpu.VMEM((ni, depth, ROWS, LANES), F32)
    short = pltpu.VMEM((4, depth, ROWS, LANES), F32)
    chunks, parts = ni // CHUNK, (ni - 4) // PART
    slots = jax.ShapeDtypeStruct((8, depth, ROWS, LANES), F32)
    return pl.pallas_call(
        inner_kernel,
        out_shape=(
            jax.ShapeDtypeStruct((ni, nx, nz), F32),
            jax.ShapeDtypeStruct((3, ni, nx, nz), F32),
            jax.ShapeDtypeStruct((4, 8, LANES), F32),
        )
        + (slots,) * len(HANDED),
        in_specs=[pl.BlockSpec(memory_space=pltpu.SMEM)]
        + [pl.BlockSpec(memory_space=HBM)] * 2
        + [pl.BlockSpec(memory_space=VMEM)] * 2,
        out_specs=[pl.BlockSpec(memory_space=HBM)] * 2
        + [pl.BlockSpec(memory_space=VMEM)] * (1 + len(HANDED)),
        scratch_shapes=[pltpu.VMEM((ni, nx, nz), F32)] * 2
        + [full] * 2
        + [short] * 6
        + [
            pltpu.VMEM((ni, nx, nz), F32),
            pltpu.VMEM((3, ni, nx, nz), F32),
            pltpu.SemaphoreType.DMA((2, chunks)),
            pltpu.SemaphoreType.DMA((parts,)),
            pltpu.SemaphoreType.DMA((3, parts)),
        ],
        compiler_params=pltpu.CompilerParams(vmem_limit_bytes=42 << 20),
        cost_estimate=pl.CostEstimate(flops=200_000_000, transcendentals=0, bytes_accessed=12 << 20),
        name="inner_planes",
    )(flags, noisy, bound, halo_n, halo_b)


def edge_kernel(flags, got_a, got_c, n4_ref, b4_ref, hb, sums_ref, *refs):
    given = dict(zip([name for name, _ in HANDED], refs))
    refs = refs[len(HANDED) :]
    _, _, u_hbm, d_hbm, spread_ref = refs[:5]
    ve, ue, di, dx, dz, div1, di2, dx2, uo, do, u_sems, d_sems = refs[5:]
    own = dict(ve=ve, ue=ue, di=di, dx=dx, dz=dz, div1=div1, di2=di2)
    depth, ni = got_a.shape[0], u_hbm.shape[0]
    more_i, more_x, even_i = flags[0] > 0, flags[1] > 0, flags[2] == 0

    def up(j, row):
        rows = pl.ds(row, 8)
        return jnp.where(even_i, got_c[j, rows, :], got_a[j, rows, :])

    def down(j, row):
        rows = pl.ds(row, 8)
        return jnp.where(even_i, got_a[j, rows, :], got_c[j, rows, :])

    def bound_of(p, j, s):
        if p == 0:
            return up(j, 40 + 8 * s)
        return hb[boundary_planes(ni)[KEPT[p]], j, 0:8, :] if s == 4 else tile(b4_ref, KEPT[p], j, s)

    t = Fields(
        lambda p: p,
        dx2=dx2,
        bound_of=bound_of,
        image_of=lambda p, j, s: tile(n4_ref, KEPT[p], j, s),
        **{name: Split(given[name], own[name], slots) for name, slots in HANDED},
    )
    a = sums_ref[0], sums_ref[1]
    b = sums_ref[2], sums_ref[3]

    for j in range(depth):
        for s in range(5):
            t.ve[0, j, strip(s), :] = SIGMA * up(j, 8 * s)
            t.ve[7, j, strip(s), :] = jnp.where(
                more_i, SIGMA * down(j, 8 * s), t.ve[6, j, strip(s), :]
            )
    for j in range(depth):
        for s in range(5):
            low = clip(t.ve[1, j, strip(s), :] - t.ve[0, j, strip(s), :], up(j, 40 + 8 * s))
            t.di[0, j, strip(s), :] = low
            if s < 4:
                part = up(j, 80 + 8 * s)
                t.ue[0, j, strip(s), :] = t.ve[0, j, strip(s), :] + TWO_CS * (part + low)
    a = first(t, 1, depth, more_x, a)
    for s in range(4):
        for j in range(depth):
            second_i(t, 0, s, j)
    b = second(t, 1, 0, depth, b, uo, do)
    b = second(t, 2, 1, depth, b, uo, do)

    def writes(k, plane):
        at, to = pl.ds(2 * k, 2), pl.ds(plane, 2)
        return [pltpu.make_async_copy(uo.at[at], u_hbm.at[to], u_sems.at[k])] + [
            pltpu.make_async_copy(do.at[c, at], d_hbm.at[c, to], d_sems.at[c, k]) for c in range(3)
        ]

    copies = writes(0, 0)
    for copy in copies:
        copy.start()
    a = first(t, 6, depth, more_x, a)
    for j in range(depth):
        for s in range(4):
            part = down(j, 40 + 8 * s)
            top = t.ve[7, j, strip(s), :] + TWO_CS * (part - t.di[6, j, strip(s), :])
            t.ue[7, j, strip(s), :] = jnp.where(more_i, top, t.ue[6, j, strip(s), :])
    b = second(t, 5, 2, depth, b, uo, do)
    b = second(t, 6, 3, depth, b, uo, do)
    last = writes(1, ni - 2)
    for copy in last:
        copy.start()
    factors = (C * C, 1.0, C * C, 1.0)
    lane = lax.broadcasted_iota(jnp.int32, (1, 4), 1)
    row = jnp.zeros((1, 4), F32)
    for k, total in enumerate(a + b):
        row = jnp.where(lane == k, factors[k] * jnp.sum(total), row)
    spread_ref[...] = jnp.broadcast_to(row, spread_ref.shape)
    for copy in copies + last:
        copy.wait()


def edges(flags, got_a, got_c, n4, b4, halo_b, sums, handed, primal, dual, devices):
    _, nx, nz = primal.shape
    depth = nz // LANES
    buffer = pltpu.VMEM((8, depth, ROWS, LANES), F32)
    count = 7 + len(handed)
    return pl.pallas_call(
        edge_kernel,
        out_shape=(
            jax.ShapeDtypeStruct(primal.shape, F32),
            jax.ShapeDtypeStruct(dual.shape, F32),
            jax.ShapeDtypeStruct((devices, 4), F32),
        ),
        in_specs=[pl.BlockSpec(memory_space=pltpu.SMEM)]
        + [pl.BlockSpec(memory_space=VMEM)] * (count - 1)
        + [pl.BlockSpec(memory_space=HBM)] * 2,
        out_specs=[pl.BlockSpec(memory_space=HBM)] * 2 + [pl.BlockSpec(memory_space=VMEM)],
        scratch_shapes=[buffer] * 8
        + [
            pltpu.VMEM((4, nx, nz), F32),
            pltpu.VMEM((3, 4, nx, nz), F32),
            pltpu.SemaphoreType.DMA((2,)),
            pltpu.SemaphoreType.DMA((3, 2)),
        ],
        input_output_aliases={count: 0, count + 1: 1},
        compiler_params=pltpu.CompilerParams(vmem_limit_bytes=24 << 20),
        name="edge_planes",
    )(flags, got_a, got_c, n4, b4, halo_b, sums, *handed, primal, dual)


def per_device(noisy, bound):
    count_i, count_x = lax.axis_size("inl"), lax.axis_size("xln")
    at_i, at_x = lax.axis_index("inl"), lax.axis_index("xln")
    flags = jnp.stack(
        [
            (at_i < count_i - 1).astype(jnp.int32),
            (at_x < count_x - 1).astype(jnp.int32),
            at_i % 2,
            at_x % 2,
        ]
    )
    noisy, bound = (pltpu.with_memory_space_constraint(x, HBM) for x in (noisy, bound))
    send_a, send_c, n4, b4 = pack(flags, noisy, bound)
    got_c = swapped(send_c, "xln", 1)
    got_a = swapped(send_a, "xln", 0)
    face_a, face_c, halo_n, halo_b = planes(flags, n4, b4, send_a, send_c, got_a, got_c)
    back_a = swapped(face_a, "inl", 0)
    back_c = swapped(face_c, "inl", 1)
    primal, dual, sums, *handed = inner(flags, noisy, bound, halo_n, halo_b)
    primal, dual, spread = edges(
        flags, back_a, back_c, n4, b4, halo_b, sums, handed, primal, dual, count_i * count_x
    )
    parts = lax.all_to_all(spread, AXES, 0, 0, tiled=True)
    norms = jnp.sqrt(jnp.sum(parts, axis=0)).reshape(2, 2)
    return primal, dual, norms


def solution(mesh):
    in_specs = (P("inl", "xln", None), P("inl", "xln", None))
    out_specs = (P("inl", "xln", None), P(None, "inl", "xln", None), P())
    return jax.shard_map(
        per_device, mesh=mesh, in_specs=in_specs, out_specs=out_specs, check_vma=False
    )
```

time: 119 us -> 62.5 us (0.53)
  other arithmetic: 34.7 us -> 0.36 us
  Pallas kernels: 0 us -> 19.3 us
  blocking collectives: 48.2 us -> 29.2 us
  starting transfers between devices: 23.4 us -> 5.96 us
  between operations: 4.58 us -> 0.73 us
  local copies, waits for them, and re-layouts: 3.87 us -> 0.66 us
  waiting for transfers between devices: 3.63 us -> 6.05 us
    psum x4 -> x0, blocking collectives: 48.2 us -> none  [over_axes(): return functools.reduce(lax.psum, axes, shard)]
    all_to_all x0 -> x1, blocking collectives: none -> 29.2 us  [per_device(): parts = lax.all_to_all(spread, AXES, 0, 0, tiled=True)]
    pallas_call x0 -> x4, Pallas kernels: none -> 19.3 us  [the longest x1 13.4 us: inner(): pl.pallas_call(inner_kernel, out_shape=(jax.ShapeDtypeStruct((ni, nx, nz)...]
    ppermute x8 -> x4, starting transfers between devices: 23.4 us -> 5.96 us  [swapped(): return lax.ppermute(value, axis, pairs)]
    sub x7 -> x0, other arithmetic: 12.4 us -> none  [the longest x2 4.41 us: per_device(): smooth[:, 1:] - smooth[:, :-1]]
    reduce_sum x2 -> x1, other arithmetic: 11 us -> 0.29 us  [per_device(): norms = jnp.sqrt(jnp.sum(parts, axis=0)).reshape(2, 2)]
    min x1 -> x0, other arithmetic: 4.53 us -> none  [per_device(): fresh_i = jnp.clip(dual_i + SIGMA * grad_i, -bound, bound)]
    another operation x2 -> x1, other arithmetic: 4 us -> 0.08 us  [per_device(): jnp.stack([(at_i < count_i - 1).astype(jnp.int32), (at_x < count_x - 1).a...]
  transfers between devices with their start and end apart: 8 -> 4, of which waited for: 3 -> 1; matrix products, arithmetic and copies ran while one was open for 12% -> 0% of each run, Pallas kernels for 0% -> 21%
where the time goes in v2:
time: 62.5 us; the launch traced here: 62.3 us
  blocking collectives  29.2 us (47%)
  Pallas kernels  19.3 us (31%)
  waiting for transfers between devices  6.05 us (10%)
  starting transfers between devices  5.96 us (10%)
  between operations  0.73 us (1%)
  local copies, waits for them, and re-layouts  0.66 us (1%)
    all_to_all x1, blocking collectives, per_device(): parts = lax.all_to_all(spread, AXES, 0, 0, tiled=True)  29.2 us
    pallas_call x1, Pallas kernels, inner(): pl.pallas_call(inner_kernel, out_shape=(jax.ShapeDtypeStruct((ni, nx, nz)...  13.4 us
    ppermute x4, waiting for transfers between devices, swapped(): return lax.ppermute(value, axis, pairs)  6.05 us
    ppermute x4, starting transfers between devices, swapped(): return lax.ppermute(value, axis, pairs)  5.96 us
    pallas_call x1, Pallas kernels, pack(): pl.pallas_call(pack_kernel, out_shape=(message, message, boundary, bounda...  2.68 us
    pallas_call x1, Pallas kernels, edges(): pl.pallas_call(edge_kernel, out_shape=(jax.ShapeDtypeStruct(primal.shape,...  2.17 us
  transfers between devices with their start and end apart: 4, of which 1 were waited for; matrix products, arithmetic and copies ran while one was open for 0% of the time, Pallas kernels for 21%

profile of v2, /device:TPU:1, one launch (start us, length us, event | category | flops | bytes accessed | tf_op | source)
XLA Modules:
  0.0 62.3 jit_solution(5559149774434260671)
XLA Ops:
  0.7 0.1 pad_add_fusion.flags
  0.7 2.7 %pack_faces.1 = (f32[32,4,4,128]{3,2,1,0:T(4,128)S(1)}, f32[32,4,4,128]{3,2,1,0:T(4,128)S(1)}, f32[4,32,512]{2,1,0:T(8,128)S(1)}, f32[4,32,512]{2,1,0:T(8,128)S(1)}) custom-call(s32[4]{0:T(128)S(1)} %pad_add_fusion.flags, f32[32,32,512]{2,1,0:T(8,128)} %n_hbm.3, f32[32,32,512]{2,1,0:T(8,128)} %b_hbm.3), custom_call_target="tpu_custom_call" | custom-call | tf_op jit(solution)/shard_map/pack_faces/pallas_call | solution.py:102
  3.4 3.3 %collective-permute-start = (f32[32,4,4,128]{3,2,1,0:T(4,128)S(1)}, f32[32,4,4,128]{3,2,1,0:T(4,128)S(1)}, u32[]{:S(2)}, u32[]{:S(2)}) collective-permute-start(f32[32,4,4,128]{3,2,1,0:T(4,128)S(1)} %get-tuple-element.26.sent_a), channel_id=1, source_target_pairs={{0,1},{1,0},{2,3},{3,2},{4,5},{5,4},{6,7},{7,6},{8,9},{9,8},{10,11... | collective-permute-start | bytes 786440 | tf_op jit(solution)/shard_map/ppermute | solution.py:27
  6.7 1.9 %collective-permute-start.1 = (f32[32,4,4,128]{3,2,1,0:T(4,128)S(1)}, f32[32,4,4,128]{3,2,1,0:T(4,128)S(1)}, u32[]{:S(2)}, u32[]{:S(2)}) collective-permute-start(f32[32,4,4,128]{3,2,1,0:T(4,128)S(1)} %get-tuple-element.27.sent_c), channel_id=1, source_target_pairs={{1,2},{2,1},{3,4},{4,3},{5,6},{6,5},{7,8},{8,7},{9,10},{10,9},{11,... | collective-permute-start | bytes 786440 | tf_op jit(solution)/shard_map/ppermute | solution.py:27
  8.6 0.0 collective-permute-done.got_a
  8.6 6.0 %collective-permute-done.1.got_c = f32[32,4,4,128]{3,2,1,0:T(4,128)S(1)} collective-permute-done((f32[32,4,4,128]{3,2,1,0:T(4,128)S(1)}, f32[32,4,4,128]{3,2,1,0:T(4,128)S(1)}, u32[]{:S(2)}, u32[]{:S(2)}) %collective-permute-start.1) | collective-permute-done | bytes 262176 | tf_op jit(solution)/shard_map/ppermute | solution.py:27
  14.7 1.1 %pack_planes.1 = (f32[4,112,128]{2,1,0:T(8,128)S(1)}, f32[4,112,128]{2,1,0:T(8,128)S(1)}, f32[32,4,8,128]{3,2,1,0:T(8,128)S(1)}, f32[32,4,8,128]{3,2,1,0:T(8,128)S(1)}) custom-call(s32[4]{0:T(128)S(1)} %pad_add_fusion.flags, f32[4,32,512]{2,1,0:T(8,128)S(1)} %get-tuple-element.24.n4_ref, f32[4,32,512]{2,1,0:T(8,128)S(1)} %get-tuple-element.25.b4_ref, ...), custom_call_target="tpu_custom_call" | custom-call | tf_op jit(solution)/shard_map/pack_planes/pallas_call | solution.py:262
  15.8 0.1 collective-permute-start.2
  15.9 0.7 %collective-permute-start.3 = (f32[4,112,128]{2,1,0:T(8,128)S(1)}, f32[4,112,128]{2,1,0:T(8,128)S(1)}, u32[]{:S(2)}, u32[]{:S(2)}) collective-permute-start(f32[4,112,128]{2,1,0:T(8,128)S(1)} %get-tuple-element.29), channel_id=1, source_target_pairs={{32,64},{64,32},{96,128},{128,96},{160,192},{192,160},{33,65},{65,... | collective-permute-start | bytes 688136 | tf_op jit(solution)/shard_map/ppermute | solution.py:27
  16.6 13.4 %inner_planes.1 = (f32[32,32,512]{2,1,0:T(8,128)}, f32[3,32,32,512]{3,2,1,0:T(8,128)}, f32[4,8,128]{2,1,0:T(8,128)S(1)}, f32[8,4,56,128]{3,2,1,0:T(8,128)S(1)}, ...) custom-call(s32[4]{0:T(128)S(1)} %pad_add_fusion.flags, ...), custom_call_target="tpu_custom_call" | custom-call | flops 200000000 | bytes 12582912 | tf_op jit(solution)/shard_map/inner_planes/pallas_call | solution.py:496
  30.0 0.0 collective-permute-done.2.got_a
  30.0 0.0 collective-permute-done.3.got_c
  30.0 2.2 %edge_planes.1 = (f32[32,32,512]{2,1,0:T(8,128)}, f32[3,32,32,512]{3,2,1,0:T(8,128)}, f32[256,4]{1,0:T(8,128)S(1)}) custom-call(s32[4]{0:T(128)S(1)} %pad_add_fusion.flags, f32[4,112,128]{2,1,0:T(8,128)S(1)} %collective-permute-done.2.got_a, f32[4,112,128]{2,1,0:T(8,128)S(1)} %collective-permute-done.3.got_c, ...), custom_call_target="tpu_custom_call", output_to_operand_aliasing={{0}: (14, {}), {1}: (15, {})} | custom-call | tf_op jit(solution)/shard_map/edge_planes/pallas_call | solution.py:612
  32.2 29.2 %all_to_all.9 = f32[256,1,4]{2,1,0:T(1,128)S(1)} all-to-all(f32[256,1,4]{2,1,0:T(1,128)S(1)} %bitcast.7), channel_id=1, replica_groups=mesh['inl'=8,'xln'=32] {'inl','xln'}, dimensions={0} | all-to-all | bytes 8192 | tf_op jit(solution)/shard_map/all_to_all | solution.py:658
  61.3 0.3 reduce_sum.9
  61.6 0.7 %sqrt.8 = f32[2,2]{1,0:T(2,128)} reshape(f32[4]{0:T(128)S(1)} %sqrt.7) | data formatting | bytes 32 | tf_op jit(solution)/shard_map/sqrt | solution.py:659
  (1 shorter events, 0.0 us)
Async XLA Ops:
  3.4 5.2 %collective-permute-start = (f32[32,4,4,128]{3,2,1,0:T(4,128)S(1)}, f32[32,4,4,128]{3,2,1,0:T(4,128)S(1)}, u32[]{:S(2)}, u32[]{:S(2)}) collective-permute-start(f32[32,4,4,128]{3,2,1,0:T(4,128)S(1)} %get-tuple-element.26.sent_a), channel_id=1, source_target_pairs={{0,1},{1,0},{2,3},{3,2},{4,5},{5,4},{6,7},{7,6},{8,9},{9,8},{10,11... | collective-permute-start | bytes 786440 | tf_op jit(solution)/shard_map/ppermute | solution.py:27
  6.7 8.0 %collective-permute-start.1 = (f32[32,4,4,128]{3,2,1,0:T(4,128)S(1)}, f32[32,4,4,128]{3,2,1,0:T(4,128)S(1)}, u32[]{:S(2)}, u32[]{:S(2)}) collective-permute-start(f32[32,4,4,128]{3,2,1,0:T(4,128)S(1)} %get-tuple-element.27.sent_c), channel_id=1, source_target_pairs={{1,2},{2,1},{3,4},{4,3},{5,6},{6,5},{7,8},{8,7},{9,10},{10,9},{11,... | collective-permute-start | bytes 786440 | tf_op jit(solution)/shard_map/ppermute | solution.py:27
  15.8 14.2 %collective-permute-start.2 = (f32[4,112,128]{2,1,0:T(8,128)S(1)}, f32[4,112,128]{2,1,0:T(8,128)S(1)}, u32[]{:S(2)}, u32[]{:S(2)}) collective-permute-start(f32[4,112,128]{2,1,0:T(8,128)S(1)} %get-tuple-element.28), channel_id=1, source_target_pairs={{0,32},{32,0},{64,96},{96,64},{128,160},{160,128},{192,224},{224,1... | collective-permute-start | bytes 688136 | tf_op jit(solution)/shard_map/ppermute | solution.py:27
  15.9 14.1 %collective-permute-start.3 = (f32[4,112,128]{2,1,0:T(8,128)S(1)}, f32[4,112,128]{2,1,0:T(8,128)S(1)}, u32[]{:S(2)}, u32[]{:S(2)}) collective-permute-start(f32[4,112,128]{2,1,0:T(8,128)S(1)} %get-tuple-element.29), channel_id=1, source_target_pairs={{32,64},{64,32},{96,128},{128,96},{160,192},{192,160},{33,65},{65,... | collective-permute-start | bytes 688136 | tf_op jit(solution)/shard_map/ppermute | solution.py:27

commit v3 on v2

--- a/solution.py
+++ b/solution.py
@@ -56,10 +56,9 @@
     even = flags[3] == 0
     columns, planes = [], []
     for k, src in enumerate((n_hbm, b_hbm)):
-        for m, start in enumerate((jnp.where(even, nx - 8, 0), jnp.where(even, 0, nx - 8))):
-            start = pl.multiple_of(start, 8)
+        for m, start in enumerate((nx - 2, 0)):
             columns.append(
-                pltpu.make_async_copy(src.at[:, pl.ds(start, 8), :], slab.at[m, k], sems.at[m, k])
+                pltpu.make_async_copy(src.at[:, pl.ds(start, 2), :], slab.at[m, k], sems.at[m, k])
             )
     for k, (src, dst) in enumerate(((n_hbm, n4_ref), (b_hbm, b4_ref))):
         for q, i in enumerate((0, ni - 2)):
@@ -77,12 +76,9 @@
         for k in range(2):
             for j in range(depth):
                 lanes = pl.ds(j * LANES, LANES)
-                a_ref[i, j, 2 * k : 2 * k + 2, :] = jnp.where(
-                    even, slab[0, k, i, 6:8, lanes], slab[0, k, i, 0:2, lanes]
-                )
-                c_ref[i, j, 2 * k : 2 * k + 2, :] = jnp.where(
-                    even, slab[1, k, i, 0:2, lanes], slab[1, k, i, 6:8, lanes]
-                )
+                high, low = slab[0, k, i, 0:2, lanes], slab[1, k, i, 0:2, lanes]
+                a_ref[i, j, 2 * k : 2 * k + 2, :] = jnp.where(even, high, low)
+                c_ref[i, j, 2 * k : 2 * k + 2, :] = jnp.where(even, low, high)
         return 0
 
     lax.fori_loop(0, ni, body, 0, unroll=2)
@@ -105,7 +101,7 @@
         in_specs=[pl.BlockSpec(memory_space=pltpu.SMEM)] + [pl.BlockSpec(memory_space=HBM)] * 2,
         out_specs=[pl.BlockSpec(memory_space=VMEM)] * 4,
         scratch_shapes=[
-            pltpu.VMEM((2, 2, ni, 8, nz), F32),
+            pltpu.VMEM((2, 2, ni, 2, nz), F32),
             pltpu.SemaphoreType.DMA((2, 2)),
             pltpu.SemaphoreType.DMA((2, 2)),
         ],
@@ -185,7 +181,7 @@
 
 
 def planes_kernel(
-    flags, n4_ref, b4_ref, sent_a, sent_c, got_a, got_c,
+    flags, n4_ref, b4_ref, sent_a, sent_c, got_a, got_c, _,
     a_ref, c_ref, hn, hb, ve, dx,
 ):
     ni, depth = got_a.shape[0], got_a.shape[1]
@@ -256,19 +252,19 @@
         up(c_ref)
 
 
-def planes(flags, n4, b4, sent_a, sent_c, got_a, got_c):
+def planes(flags, n4, b4, sent_a, sent_c, got_a, got_c, after):
     ni, depth = got_a.shape[0], got_a.shape[1]
     buffer = pltpu.VMEM((4, depth, ROWS, LANES), F32)
     return pl.pallas_call(
         planes_kernel,
         out_shape=(pltpu.VMEM((depth, 112, LANES), F32),) * 2
         + (pltpu.VMEM((ni, depth, 8, LANES), F32),) * 2,
-        in_specs=[pl.BlockSpec(memory_space=pltpu.SMEM)] + [pl.BlockSpec(memory_space=VMEM)] * 6,
+        in_specs=[pl.BlockSpec(memory_space=pltpu.SMEM)] + [pl.BlockSpec(memory_space=VMEM)] * 7,
         out_specs=[pl.BlockSpec(memory_space=VMEM)] * 4,
         scratch_shapes=[buffer] * 2,
         compiler_params=pltpu.CompilerParams(vmem_limit_bytes=8 << 20),
         name="pack_planes",
-    )(flags, n4, b4, sent_a, sent_c, got_a, got_c)
+    )(flags, n4, b4, sent_a, sent_c, got_a, got_c, after)
 
 
 class Fields:
@@ -315,7 +311,7 @@
 def second_i(t, p, s, j):
     q = t.ring(p)
     t.di2[q, j, strip(s), :] = clip(
-        t.di[q, j, strip(s), :] + (t.ue[p + 1, j, strip(s), :] - t.ue[p, j, strip(s), :]),
+        t.di_of(p, j, s) + (t.ue[p + 1, j, strip(s), :] - t.ue[p, j, strip(s), :]),
         t.bound_of(p, j, s),
     )
 
@@ -338,7 +334,7 @@
             for j in range(depth):
                 t.dx2[q, j, pl.ds(OWN - 1, 1), :] = t.dx2[q, j, pl.ds(HALO + 7, 1), :]
             continue
-        z_old = [t.dz[q, j, strip(s), :] for j in range(depth)]
+        z_old = [t.dz_of(p, j, s) for j in range(depth)]
         z_new = [
             clip2(z_old[j] + (n - u[j]), b[j], c[j]) for j, n in enumerate(depth_next(u))
         ]
@@ -346,7 +342,7 @@
         rows = pl.ds(8 * s, 8)
         for j in range(depth):
             lanes = pl.ds(j * LANES, LANES)
-            i_old = t.di[q, j, strip(s), :]
+            i_old = t.di_of(p, j, s)
             i_new = clip2(i_old + (t.ue[p + 1, j, strip(s), :] - u[j]), b[j], c[j])
             t.di2[q, j, strip(s), :] = i_new
             total = (
@@ -388,30 +384,92 @@
 )
 
 
-def inner_kernel(flags, n_hbm, b_hbm, hn, hb, u_hbm, d_hbm, sums_ref, *refs):
-    handed, refs = refs[: len(HANDED)], refs[len(HANDED) :]
-    ne, be, ve, ue, di, dx, dz, div1, dx2, di2, uo, do, in_sems, u_sems, d_sems = refs
+def own_kernel(n_hbm, b_hbm, nv, bv, di, dz, part, sum_ref, sems):
     ni, depth = n_hbm.shape[0], n_hbm.shape[2] // LANES
-    more_x = flags[1] > 0
-
-    def bound_of(p, j, s):
-        return hb[p, j, 0:8, :] if s == 4 else tile(be, p, j, s)
-
-    def image_of(p, j, s):
-        return hn[p, j, 0:8, :] if s == 4 else tile(ne, p, j, s)
-
-    t = Fields(
-        lambda p: p % 4,
-        bound_of=bound_of, image_of=image_of, ve=ve, ue=ue, di=di, dx=dx, dz=dz, div1=div1, dx2=dx2, di2=di2,
-    )
-    chunks, parts = ni // CHUNK, (ni - 4) // PART
+    chunks = ni // CHUNK
 
     def reads(c):
         span = pl.ds(c * CHUNK, CHUNK)
         return [
-            pltpu.make_async_copy(src.at[span], dst.at[span], in_sems.at[k, c])
-            for k, (src, dst) in enumerate(((n_hbm, ne), (b_hbm, be)))
+            pltpu.make_async_copy(src.at[span], dst.at[span], sems.at[k, c])
+            for k, (src, dst) in enumerate(((n_hbm, nv), (b_hbm, bv)))
         ]
+
+    for c in range(chunks):
+        for copy in reads(c):
+            copy.start()
+    for copy in reads(0):
+        copy.wait()
+
+    def spot(j, s):
+        return pl.ds(8 * s, 8), pl.ds(j * LANES, LANES)
+
+    for s in range(4):
+        for j in range(depth):
+            gap = SIGMA * (tile(nv, 1, j, s) - tile(nv, 0, j, s))
+            di[(0,) + spot(j, s)] = clip(gap, tile(bv, 0, j, s))
+
+    def body(p, total):
+        @pl.when((p + 1) % CHUNK == 0)
+        def _():
+            for copy in reads((p + 1) // CHUNK):
+                copy.wait()
+
+        for s in range(4):
+            n = [tile(nv, p, j, s) for j in range(depth)]
+            b = [tile(bv, p, j, s) for j in range(depth)]
+            c = [-k for k in b]
+            z = [clip2(SIGMA * (m - o), k, l) for m, o, k, l in zip(depth_next(n), n, b, c)]
+            back = depth_back(z)
+            for j in range(depth):
+                new = clip2(SIGMA * (tile(nv, p + 1, j, s) - n[j]), b[j], c[j])
+                at = (p,) + spot(j, s)
+                di[at] = new
+                dz[at] = z[j]
+                part[at] = (new - tile(di, p - 1, j, s)) + (z[j] - back[j])
+                total = total + (new * new + z[j] * z[j])
+        return total
+
+    sum_ref[...] = lax.fori_loop(1, ni - 1, body, jnp.zeros((8, LANES), F32))
+
+
+def own(noisy, bound):
+    ni, nx, nz = noisy.shape
+    whole = pltpu.VMEM((ni, nx, nz), F32)
+    return pl.pallas_call(
+        own_kernel,
+        out_shape=(whole,) * 5 + (pltpu.VMEM((8, LANES), F32),),
+        in_specs=[pl.BlockSpec(memory_space=HBM)] * 2,
+        out_specs=[pl.BlockSpec(memory_space=VMEM)] * 6,
+        scratch_shapes=[pltpu.SemaphoreType.DMA((2, ni // CHUNK))],
+        compiler_params=pltpu.CompilerParams(vmem_limit_bytes=16 << 20),
+        cost_estimate=pl.CostEstimate(flops=100_000_000, transcendentals=0, bytes_accessed=4 << 20),
+        name="own_planes",
+    )(noisy, bound)
+
+
+def inner_kernel(flags, nv, bv, di, dz, part, own_sum, hn, hb, u_hbm, d_hbm, sums_ref, *refs):
+    handed, refs = refs[: len(HANDED)], refs[len(HANDED) :]
+    ve, ue, dh, dx, div1, dx2, di2, uo, do, u_sems, d_sems = refs
+    ni, depth = nv.shape[0], nv.shape[2] // LANES
+    more_x = flags[1] > 0
+    parts = (ni - 4) // PART
+
+    def bound_of(p, j, s):
+        return hb[p, j, 0:8, :] if s == 4 else tile(bv, p, j, s)
+
+    def image_of(p, j, s):
+        return hn[p, j, 0:8, :] if s == 4 else tile(nv, p, j, s)
+
+    def di_of(p, j, s):
+        return dh[p % 4, j, 0:8, :] if s == 4 else tile(di, p, j, s)
+
+    t = Fields(
+        lambda p: p % 4,
+        bound_of=bound_of, image_of=image_of, di_of=di_of,
+        dz_of=lambda p, j, s: tile(dz, p, j, s),
+        ve=ve, ue=ue, dx=dx, div1=div1, dx2=dx2, di2=di2,
+    )
 
     def writes(c):
         span = pl.ds(c * PART + 2, PART)
@@ -422,37 +480,85 @@
 
     def hand(slots):
         for ref, (name, wanted) in zip(handed, HANDED):
-            field = getattr(t, name)
-            short = name in ("di", "dx", "dz", "div1", "di2")
             for slot in wanted:
-                if slot in slots:
-                    plane = slot - 1 if slot < 4 else ni - 7 + slot
-                    place = plane % 4 if short else plane
-                    for j in range(depth):
-                        for s in range(5):
-                            if s < 4 or name not in ("dz", "div1", "di2"):
-                                ref[slot, j, strip(s), :] = field[place, j, strip(s), :]
-                        if name in ("ve", "ue"):
-                            ref[slot, j, pl.ds(HALO + 8, 1), :] = field[place, j, pl.ds(HALO + 8, 1), :]
+                if slot not in slots:
+                    continue
+                plane = slot - 1 if slot < 4 else ni - 7 + slot
+                for j in range(depth):
+                    for s in range(4 if name in ("dz", "div1", "di2") else 5):
+                        if name == "di":
+                            value = di_of(plane, j, s)
+                        elif name == "dz":
+                            value = tile(dz, plane, j, s)
+                        elif name in ("ve", "ue"):
+                            value = getattr(t, name)[plane, j, strip(s), :]
+                        else:
+                            value = getattr(t, name)[plane % 4, j, strip(s), :]
+                        ref[slot, j, strip(s), :] = value
+                    if name in ("ve", "ue"):
+                        behind = pl.ds(HALO + 8, 1)
+                        ref[slot, j, behind, :] = getattr(t, name)[plane, j, behind, :]
 
     def ready(p):
         scale(p, depth, image_of, ve)
 
-    for c in range(chunks):
-        for copy in reads(c):
-            copy.start()
-    for copy in reads(0):
-        copy.wait()
+    def halo_i(p):
+        return [
+            clip(ve[p + 1, j, strip(4), :] - ve[p, j, strip(4), :], hb[p, j, 0:8, :])
+            for j in range(depth)
+        ]
+
+    def first_inner(p, sums):
+        p1, d1 = sums
+        q = p % 4
+        for s in (3,) + ORDER[:4]:
+            v = [ve[p, j, strip(s), :] for j in range(depth)]
+            b = [bound_of(p, j, s) for j in range(depth)]
+            c = [-k for k in b]
+            x = x_dual(p, s, depth, ve, v, b, c)
+            for j in range(depth):
+                dx[q, j, strip(s), :] = x[j]
+            if s == 3:
+                continue
+            finish = [x[j] - dx[q, j, strip_back(s), :] for j in range(depth)]
+            if s == 4:
+                z = [clip2(n - o, k, m) for n, o, k, m in zip(depth_next(v), v, b, c)]
+                back = depth_back(z)
+                new = halo_i(p)
+                for j in range(depth):
+                    below = new[j] - dh[(p - 1) % 4, j, 0:8, :]
+                    dh[q, j, 0:8, :] = new[j]
+                    total = finish[j] + (z[j] - back[j]) + below
+                    ue[p, j, strip(4), :] = v[j] + TWO_CS * total
+                    dx[q, j, pl.ds(OWN - 1, 1), :] = dx[q, j, pl.ds(HALO + 7, 1), :]
+                continue
+            for j in range(depth):
+                total = finish[j] + tile(part, p, j, s)
+                ue[p, j, strip(s), :] = v[j] + TWO_CS * total
+                div1[q, j, strip(s), :] = total
+                p1 = p1 + total * total
+                d1 = d1 + x[j] * x[j]
+        s = 3
+        for j in range(depth):
+            x3 = dx[q, j, strip(s), :]
+            total = (x3 - dx[q, j, strip_back(s), :]) + tile(part, p, j, s)
+            ue[p, j, strip(s), :] = ve[p, j, strip(s), :] + TWO_CS * total
+            div1[q, j, strip(s), :] = total
+            p1 = p1 + total * total
+            d1 = d1 + x3 * x3
+        for j in range(depth):
+            edge = ue[p, j, pl.ds(HALO - 1, 1), :]
+            ue[p, j, pl.ds(HALO, 1), :] = jnp.where(more_x, ue[p, j, pl.ds(HALO, 1), :], edge)
+        wrap_rows(ue, p, depth)
+        return p1, d1
+
     for p in range(4):
         ready(p)
-    for j in range(depth):
-        for s in range(5):
-            di[0, j, strip(s), :] = clip(
-                ve[1, j, strip(s), :] - ve[0, j, strip(s), :], bound_of(0, j, s)
-            )
+    for j, value in enumerate(halo_i(0)):
+        dh[0, j, 0:8, :] = value
     zero = jnp.zeros((8, LANES), F32)
-    a = first(t, 1, depth, more_x, (zero, zero))
-    a = first(t, 2, depth, more_x, a)
+    a = first_inner(1, (zero, own_sum[...]))
+    a = first_inner(2, a)
     for s in range(4):
         for j in range(depth):
             second_i(t, 1, s, j)
@@ -460,14 +566,8 @@
 
     def body(p, carry):
         a, b = carry
-
-        @pl.when((p + 1) % CHUNK == 0)
-        def _():
-            for copy in reads((p + 1) // CHUNK):
-                copy.wait()
-
         ready(p + 1)
-        a = first(t, p, depth, more_x, a)
+        a = first_inner(p, a)
         b = second(t, p - 1, p - 1, depth, b, uo, do)
 
         @pl.when(p % PART == 0)
@@ -486,40 +586,37 @@
             copy.wait()
 
 
-def inner(flags, noisy, bound, halo_n, halo_b):
-    ni, nx, nz = noisy.shape
+def inner(flags, nv, bv, di, dz, part, own_sum, halo_n, halo_b):
+    ni, nx, nz = nv.shape
     depth = nz // LANES
     full = pltpu.VMEM((ni, depth, ROWS, LANES), F32)
     short = pltpu.VMEM((4, depth, ROWS, LANES), F32)
-    chunks, parts = ni // CHUNK, (ni - 4) // PART
-    slots = jax.ShapeDtypeStruct((8, depth, ROWS, LANES), F32)
+    parts = (ni - 4) // PART
+    slots = pltpu.VMEM((8, depth, ROWS, LANES), F32)
     return pl.pallas_call(
         inner_kernel,
         out_shape=(
             jax.ShapeDtypeStruct((ni, nx, nz), F32),
             jax.ShapeDtypeStruct((3, ni, nx, nz), F32),
-            jax.ShapeDtypeStruct((4, 8, LANES), F32),
+            pltpu.VMEM((4, 8, LANES), F32),
         )
         + (slots,) * len(HANDED),
-        in_specs=[pl.BlockSpec(memory_space=pltpu.SMEM)]
-        + [pl.BlockSpec(memory_space=HBM)] * 2
-        + [pl.BlockSpec(memory_space=VMEM)] * 2,
+        in_specs=[pl.BlockSpec(memory_space=pltpu.SMEM)] + [pl.BlockSpec(memory_space=VMEM)] * 8,
         out_specs=[pl.BlockSpec(memory_space=HBM)] * 2
         + [pl.BlockSpec(memory_space=VMEM)] * (1 + len(HANDED)),
-        scratch_shapes=[pltpu.VMEM((ni, nx, nz), F32)] * 2
-        + [full] * 2
-        + [short] * 6
+        scratch_shapes=[full] * 2
+        + [pltpu.VMEM((4, depth, 8, LANES), F32)]
+        + [short] * 4
         + [
             pltpu.VMEM((ni, nx, nz), F32),
             pltpu.VMEM((3, ni, nx, nz), F32),
-            pltpu.SemaphoreType.DMA((2, chunks)),
             pltpu.SemaphoreType.DMA((parts,)),
             pltpu.SemaphoreType.DMA((3, parts)),
         ],
-        compiler_params=pltpu.CompilerParams(vmem_limit_bytes=42 << 20),
+        compiler_params=pltpu.CompilerParams(vmem_limit_bytes=24 << 20),
         cost_estimate=pl.CostEstimate(flops=200_000_000, transcendentals=0, bytes_accessed=12 << 20),
         name="inner_planes",
-    )(flags, noisy, bound, halo_n, halo_b)
+    )(flags, nv, bv, di, dz, part, own_sum, halo_n, halo_b)
 
 
 def edge_kernel(flags, got_a, got_c, n4_ref, b4_ref, hb, sums_ref, *refs):
@@ -549,6 +646,8 @@
         dx2=dx2,
         bound_of=bound_of,
         image_of=lambda p, j, s: tile(n4_ref, KEPT[p], j, s),
+        di_of=lambda p, j, s: t.di[p, j, strip(s), :],
+        dz_of=lambda p, j, s: t.dz[p, j, strip(s), :],
         **{name: Split(given[name], own[name], slots) for name, slots in HANDED},
     )
     a = sums_ref[0], sums_ref[1]
@@ -648,10 +747,13 @@
     send_a, send_c, n4, b4 = pack(flags, noisy, bound)
     got_c = swapped(send_c, "xln", 1)
     got_a = swapped(send_a, "xln", 0)
-    face_a, face_c, halo_n, halo_b = planes(flags, n4, b4, send_a, send_c, got_a, got_c)
+    alone = own(noisy, bound)
+    face_a, face_c, halo_n, halo_b = planes(
+        flags, n4, b4, send_a, send_c, got_a, got_c, alone[-1]
+    )
     back_a = swapped(face_a, "inl", 0)
     back_c = swapped(face_c, "inl", 1)
-    primal, dual, sums, *handed = inner(flags, noisy, bound, halo_n, halo_b)
+    primal, dual, sums, *handed = inner(flags, *alone, halo_n, halo_b)
     primal, dual, spread = edges(
         flags, back_a, back_c, n4, b4, halo_b, sums, handed, primal, dual, count_i * count_x
     )

time: 62.5 us -> 59.9 us (0.958)
  waiting for transfers between devices: 6.05 us -> 0.01 us
  Pallas kernels: 19.3 us -> 23.1 us
  blocking collectives: 29.2 us -> 27.9 us
  starting transfers between devices: 5.96 us -> 6.98 us
    pallas_call x0 -> x1, Pallas kernels: none -> 6.31 us  [own(): pl.pallas_call(own_kernel, out_shape=(whole,) * 5 + (pltpu.VMEM((8, LANES...]
    ppermute x4, waiting for transfers between devices: 6.05 us -> 0.01 us  [swapped(): return lax.ppermute(value, axis, pairs)]
    pallas_call x1, Pallas kernels: 13.4 us -> 11.5 us  [inner(): pl.pallas_call(inner_kernel, out_shape=(jax.ShapeDtypeStruct((ni, nx, nz)...]
    all_to_all x1, blocking collectives: 29.2 us -> 27.9 us  [per_device(): parts = lax.all_to_all(spread, AXES, 0, 0, tiled=True)]
    ppermute x4, starting transfers between devices: 5.96 us -> 6.98 us  [swapped(): return lax.ppermute(value, axis, pairs)]
    pallas_call x1, Pallas kernels: 2.68 us -> 1.98 us  [pack(): pl.pallas_call(pack_kernel, out_shape=(message, message, boundary, bounda...]
  transfers between devices with their start and end apart: 4 -> 4, of which waited for: 1 -> 0; matrix products, arithmetic and copies ran while one was open for 0% -> 0% of each run, Pallas kernels for 21% -> 30%
where the time goes in v3:
time: 59.9 us; the launch traced here: 59.7 us
  blocking collectives  27.9 us (47%)
  Pallas kernels  23.1 us (39%)
  starting transfers between devices  6.98 us (12%)
  between operations  0.74 us (1%)
  local copies, waits for them, and re-layouts  0.66 us (1%)
    all_to_all x1, blocking collectives, per_device(): parts = lax.all_to_all(spread, AXES, 0, 0, tiled=True)  27.9 us
    pallas_call x1, Pallas kernels, inner(): pl.pallas_call(inner_kernel, out_shape=(jax.ShapeDtypeStruct((ni, nx, nz)...  11.5 us
    ppermute x4, starting transfers between devices, swapped(): return lax.ppermute(value, axis, pairs)  6.98 us
    pallas_call x1, Pallas kernels, own(): pl.pallas_call(own_kernel, out_shape=(whole,) * 5 + (pltpu.VMEM((8, LANES...  6.31 us
    pallas_call x1, Pallas kernels, edges(): pl.pallas_call(edge_kernel, out_shape=(jax.ShapeDtypeStruct(primal.shape,...  2.18 us
    pallas_call x1, Pallas kernels, pack(): pl.pallas_call(pack_kernel, out_shape=(message, message, boundary, bounda...  1.98 us
  transfers between devices with their start and end apart: 4, of which 0 were waited for; matrix products, arithmetic and copies ran while one was open for 0% of the time, Pallas kernels for 30%

profile of v3, /device:TPU:1, one launch (start us, length us, event | category | flops | bytes accessed | tf_op | source)
XLA Modules:
  0.0 59.7 jit_solution(7550029052313879864)
XLA Ops:
  0.7 0.1 pad_add_fusion.flags
  0.7 2.0 %pack_faces.1 = (f32[32,4,4,128]{3,2,1,0:T(4,128)S(1)}, f32[32,4,4,128]{3,2,1,0:T(4,128)S(1)}, f32[4,32,512]{2,1,0:T(8,128)S(1)}, f32[4,32,512]{2,1,0:T(8,128)S(1)}) custom-call(s32[4]{0:T(128)S(1)} %pad_add_fusion.flags, f32[32,32,512]{2,1,0:T(8,128)} %n_hbm.3, f32[32,32,512]{2,1,0:T(8,128)} %b_hbm.3), custom_call_target="tpu_custom_call" | custom-call | tf_op jit(solution)/shard_map/pack_faces/pallas_call | solution.py:98
  2.7 3.3 %collective-permute-start = (f32[32,4,4,128]{3,2,1,0:T(4,128)S(1)}, f32[32,4,4,128]{3,2,1,0:T(4,128)S(1)}, u32[]{:S(2)}, u32[]{:S(2)}) collective-permute-start(f32[32,4,4,128]{3,2,1,0:T(4,128)S(1)} %get-tuple-element.32.sent_a), channel_id=1, source_target_pairs={{0,1},{1,0},{2,3},{3,2},{4,5},{5,4},{6,7},{7,6},{8,9},{9,8},{10,11... | collective-permute-start | bytes 786440 | tf_op jit(solution)/shard_map/ppermute | solution.py:27
  6.0 1.9 %collective-permute-start.1 = (f32[32,4,4,128]{3,2,1,0:T(4,128)S(1)}, f32[32,4,4,128]{3,2,1,0:T(4,128)S(1)}, u32[]{:S(2)}, u32[]{:S(2)}) collective-permute-start(f32[32,4,4,128]{3,2,1,0:T(4,128)S(1)} %get-tuple-element.33.sent_c), channel_id=1, source_target_pairs={{1,2},{2,1},{3,4},{4,3},{5,6},{6,5},{7,8},{8,7},{9,10},{10,9},{11,... | collective-permute-start | bytes 786440 | tf_op jit(solution)/shard_map/ppermute | solution.py:27
  7.9 6.3 %own_planes.1 = (f32[32,32,512]{2,1,0:T(8,128)S(1)}, f32[32,32,512]{2,1,0:T(8,128)S(1)}, f32[32,32,512]{2,1,0:T(8,128)S(1)}, f32[32,32,512]{2,1,0:T(8,128)S(1)},...) custom-call(f32[32,32,512]{2,1,0:T(8,128)} %n_hbm.3, f32[32,32,512]{2,1,0:T(8,128)} %b_hbm.3), custom_call_target="tpu_custom_call" | custom-call | flops 100000000 | bytes 4194304 | tf_op jit(solution)/shard_map/own_planes/pallas_call | solution.py:439
  14.2 0.0 collective-permute-done.got_a
  14.3 0.0 collective-permute-done.1.got_c
  14.3 1.1 %pack_planes.1 = (f32[4,112,128]{2,1,0:T(8,128)S(1)}, f32[4,112,128]{2,1,0:T(8,128)S(1)}, f32[32,4,8,128]{3,2,1,0:T(8,128)S(1)}, f32[32,4,8,128]{3,2,1,0:T(8,128)S(1)}) custom-call(s32[4]{0:T(128)S(1)} %pad_add_fusion.flags, f32[4,32,512]{2,1,0:T(8,128)S(1)} %get-tuple-element.30.n4_ref, f32[4,32,512]{2,1,0:T(8,128)S(1)} %get-tuple-element.31.b4_ref, ...), custom_call_target="tpu_custom_call" | custom-call | tf_op jit(solution)/shard_map/pack_planes/pallas_call | solution.py:258
  15.4 1.1 %collective-permute-start.2 = (f32[4,112,128]{2,1,0:T(8,128)S(1)}, f32[4,112,128]{2,1,0:T(8,128)S(1)}, u32[]{:S(2)}, u32[]{:S(2)}) collective-permute-start(f32[4,112,128]{2,1,0:T(8,128)S(1)} %get-tuple-element.35), channel_id=1, source_target_pairs={{0,32},{32,0},{64,96},{96,64},{128,160},{160,128},{192,224},{224,1... | collective-permute-start | bytes 688136 | tf_op jit(solution)/shard_map/ppermute | solution.py:27
  16.5 0.7 %collective-permute-start.3 = (f32[4,112,128]{2,1,0:T(8,128)S(1)}, f32[4,112,128]{2,1,0:T(8,128)S(1)}, u32[]{:S(2)}, u32[]{:S(2)}) collective-permute-start(f32[4,112,128]{2,1,0:T(8,128)S(1)} %get-tuple-element.36), channel_id=1, source_target_pairs={{32,64},{64,32},{96,128},{128,96},{160,192},{192,160},{33,65},{65,... | collective-permute-start | bytes 688136 | tf_op jit(solution)/shard_map/ppermute | solution.py:27
  17.2 11.5 %inner_planes.1 = (f32[32,32,512]{2,1,0:T(8,128)}, f32[3,32,32,512]{3,2,1,0:T(8,128)}, f32[4,8,128]{2,1,0:T(8,128)S(1)}, f32[8,4,56,128]{3,2,1,0:T(8,128)S(1)}, ...) custom-call(s32[4]{0:T(128)S(1)} %pad_add_fusion.flags, ...), custom_call_target="tpu_custom_call" | custom-call | flops 200000000 | bytes 12582912 | tf_op jit(solution)/shard_map/inner_planes/pallas_call | solution.py:596
  28.7 0.0 collective-permute-done.2.got_a
  28.7 0.0 collective-permute-done.3.got_c
  28.7 2.2 %edge_planes.1 = (f32[32,32,512]{2,1,0:T(8,128)}, f32[3,32,32,512]{3,2,1,0:T(8,128)}, f32[256,4]{1,0:T(8,128)S(1)}) custom-call(s32[4]{0:T(128)S(1)} %pad_add_fusion.flags, f32[4,112,128]{2,1,0:T(8,128)S(1)} %collective-permute-done.2.got_a, f32[4,112,128]{2,1,0:T(8,128)S(1)} %collective-permute-done.3.got_c, ...), custom_call_target="tpu_custom_call", output_to_operand_aliasing={{0}: (14, {}), {1}: (15, {})} | custom-call | tf_op jit(solution)/shard_map/edge_planes/pallas_call | solution.py:711
  30.9 27.9 %all_to_all.9 = f32[256,1,4]{2,1,0:T(1,128)S(1)} all-to-all(f32[256,1,4]{2,1,0:T(1,128)S(1)} %bitcast.7), channel_id=1, replica_groups=mesh['inl'=8,'xln'=32] {'inl','xln'}, dimensions={0} | all-to-all | bytes 8192 | tf_op jit(solution)/shard_map/all_to_all | solution.py:760
  58.8 0.3 reduce_sum.9
  59.1 0.7 %sqrt.8 = f32[2,2]{1,0:T(2,128)} reshape(f32[4]{0:T(128)S(1)} %sqrt.7) | data formatting | bytes 32 | tf_op jit(solution)/shard_map/sqrt | solution.py:761
  (1 shorter events, 0.0 us)
Async XLA Ops:
  2.7 11.5 %collective-permute-start = (f32[32,4,4,128]{3,2,1,0:T(4,128)S(1)}, f32[32,4,4,128]{3,2,1,0:T(4,128)S(1)}, u32[]{:S(2)}, u32[]{:S(2)}) collective-permute-start(f32[32,4,4,128]{3,2,1,0:T(4,128)S(1)} %get-tuple-element.32.sent_a), channel_id=1, source_target_pairs={{0,1},{1,0},{2,3},{3,2},{4,5},{5,4},{6,7},{7,6},{8,9},{9,8},{10,11... | collective-permute-start | bytes 786440 | tf_op jit(solution)/shard_map/ppermute | solution.py:27
  6.0 8.2 %collective-permute-start.1 = (f32[32,4,4,128]{3,2,1,0:T(4,128)S(1)}, f32[32,4,4,128]{3,2,1,0:T(4,128)S(1)}, u32[]{:S(2)}, u32[]{:S(2)}) collective-permute-start(f32[32,4,4,128]{3,2,1,0:T(4,128)S(1)} %get-tuple-element.33.sent_c), channel_id=1, source_target_pairs={{1,2},{2,1},{3,4},{4,3},{5,6},{6,5},{7,8},{8,7},{9,10},{10,9},{11,... | collective-permute-start | bytes 786440 | tf_op jit(solution)/shard_map/ppermute | solution.py:27
  15.4 13.3 %collective-permute-start.2 = (f32[4,112,128]{2,1,0:T(8,128)S(1)}, f32[4,112,128]{2,1,0:T(8,128)S(1)}, u32[]{:S(2)}, u32[]{:S(2)}) collective-permute-start(f32[4,112,128]{2,1,0:T(8,128)S(1)} %get-tuple-element.35), channel_id=1, source_target_pairs={{0,32},{32,0},{64,96},{96,64},{128,160},{160,128},{192,224},{224,1... | collective-permute-start | bytes 688136 | tf_op jit(solution)/shard_map/ppermute | solution.py:27
  16.5 12.2 %collective-permute-start.3 = (f32[4,112,128]{2,1,0:T(8,128)S(1)}, f32[4,112,128]{2,1,0:T(8,128)S(1)}, u32[]{:S(2)}, u32[]{:S(2)}) collective-permute-start(f32[4,112,128]{2,1,0:T(8,128)S(1)} %get-tuple-element.36), channel_id=1, source_target_pairs={{32,64},{64,32},{96,128},{128,96},{160,192},{192,160},{33,65},{65,... | collective-permute-start | bytes 688136 | tf_op jit(solution)/shard_map/ppermute | solution.py:27

commit v4 on v3

--- a/solution.py
+++ b/solution.py
@@ -27,6 +27,13 @@
     return lax.ppermute(value, axis, pairs)
 
 
+def place():
+    i, x = lax.axis_index("inl"), lax.axis_index("xln")
+    more_i = i < lax.axis_size("inl") - 1
+    more_x = x < lax.axis_size("xln") - 1
+    return more_i, more_x, lax.rem(i, 2) == 0, lax.rem(x, 2) == 0
+
+
 def clip(value, bound):
     return jnp.minimum(jnp.maximum(value, -bound), bound)
 
@@ -51,9 +58,9 @@
     return [jnp.where(mask, rolled[j], rolled[j + 1]) for j in range(len(tiles))]
 
 
-def pack_kernel(flags, n_hbm, b_hbm, a_ref, c_ref, n4_ref, b4_ref, slab, sems, plane_sems):
+def pack_kernel(n_hbm, b_hbm, a_ref, c_ref, n4_ref, b4_ref, slab, sems, plane_sems):
     ni, nx, depth = n_hbm.shape[0], n_hbm.shape[1], n_hbm.shape[2] // LANES
-    even = flags[3] == 0
+    even = place()[3]
     columns, planes = [], []
     for k, src in enumerate((n_hbm, b_hbm)):
         for m, start in enumerate((nx - 2, 0)):
@@ -90,7 +97,7 @@
 VMEM = pltpu.MemorySpace.VMEM
 
 
-def pack(flags, noisy, bound):
+def pack(noisy, bound):
     ni, nx, nz = noisy.shape
     depth = nz // LANES
     message = pltpu.VMEM((ni, depth, 4, LANES), F32)
@@ -98,7 +105,7 @@
     return pl.pallas_call(
         pack_kernel,
         out_shape=(message, message, boundary, boundary),
-        in_specs=[pl.BlockSpec(memory_space=pltpu.SMEM)] + [pl.BlockSpec(memory_space=HBM)] * 2,
+        in_specs=[pl.BlockSpec(memory_space=HBM)] * 2,
         out_specs=[pl.BlockSpec(memory_space=VMEM)] * 4,
         scratch_shapes=[
             pltpu.VMEM((2, 2, ni, 2, nz), F32),
@@ -107,7 +114,7 @@
         ],
         compiler_params=pltpu.CompilerParams(vmem_limit_bytes=8 << 20),
         name="pack_faces",
-    )(flags, noisy, bound)
+    )(noisy, bound)
 
 
 def strip(s):
@@ -181,11 +188,11 @@
 
 
 def planes_kernel(
-    flags, n4_ref, b4_ref, sent_a, sent_c, got_a, got_c, _,
+    n4_ref, b4_ref, sent_a, sent_c, got_a, got_c, _,
     a_ref, c_ref, hn, hb, ve, dx,
 ):
     ni, depth = got_a.shape[0], got_a.shape[1]
-    more_x, even_x, even_i = flags[1] > 0, flags[3] == 0, flags[2] == 0
+    _, more_x, even_i, even_x = place()
 
     def sort(i, _):
         for j in range(depth):
@@ -201,13 +208,13 @@
         return 0
 
     lax.fori_loop(0, ni, sort, 0, unroll=2)
-    place = (0, 1, ni - 2, ni - 1)
+    planes_at = (0, 1, ni - 2, ni - 1)
 
     def image_of(q, j, s):
-        return hn[place[q], j, 0:8, :] if s == 4 else tile(n4_ref, q, j, s)
+        return hn[planes_at[q], j, 0:8, :] if s == 4 else tile(n4_ref, q, j, s)
 
     def bound_of(q, j, s):
-        return hb[place[q], j, 0:8, :] if s == 4 else tile(b4_ref, q, j, s)
+        return hb[planes_at[q], j, 0:8, :] if s == 4 else tile(b4_ref, q, j, s)
 
     for q in range(4):
         scale(q, depth, image_of, ve)
@@ -252,19 +259,19 @@
         up(c_ref)
 
 
-def planes(flags, n4, b4, sent_a, sent_c, got_a, got_c, after):
+def planes(n4, b4, sent_a, sent_c, got_a, got_c, after):
     ni, depth = got_a.shape[0], got_a.shape[1]
     buffer = pltpu.VMEM((4, depth, ROWS, LANES), F32)
     return pl.pallas_call(
         planes_kernel,
         out_shape=(pltpu.VMEM((depth, 112, LANES), F32),) * 2
         + (pltpu.VMEM((ni, depth, 8, LANES), F32),) * 2,
-        in_specs=[pl.BlockSpec(memory_space=pltpu.SMEM)] + [pl.BlockSpec(memory_space=VMEM)] * 7,
+        in_specs=[pl.BlockSpec(memory_space=VMEM)] * 7,
         out_specs=[pl.BlockSpec(memory_space=VMEM)] * 4,
         scratch_shapes=[buffer] * 2,
         compiler_params=pltpu.CompilerParams(vmem_limit_bytes=8 << 20),
         name="pack_planes",
-    )(flags, n4, b4, sent_a, sent_c, got_a, got_c, after)
+    )(n4, b4, sent_a, sent_c, got_a, got_c, after)
 
 
 class Fields:
@@ -371,7 +378,7 @@
     return 0, 1, ni - 2, ni - 1
 
 
-CHUNK = 4
+GROUP = 3
 PART = 2
 HANDED = (
     ("ve", (1, 2, 5, 6)),
@@ -386,19 +393,22 @@
 
 def own_kernel(n_hbm, b_hbm, nv, bv, di, dz, part, sum_ref, sems):
     ni, depth = n_hbm.shape[0], n_hbm.shape[2] // LANES
-    chunks = ni // CHUNK
-
-    def reads(c):
-        span = pl.ds(c * CHUNK, CHUNK)
+    steps = (ni - 2) // GROUP
+
+    def reads(c, start, count):
+        span = pl.ds(start, count)
         return [
             pltpu.make_async_copy(src.at[span], dst.at[span], sems.at[k, c])
             for k, (src, dst) in enumerate(((n_hbm, nv), (b_hbm, bv)))
         ]
 
-    for c in range(chunks):
-        for copy in reads(c):
+    ahead = reads(0, 0, GROUP + 2)
+    for copy in ahead:
+        copy.start()
+    for c in range(1, steps):
+        for copy in reads(c, c * GROUP + 2, GROUP):
             copy.start()
-    for copy in reads(0):
+    for copy in ahead:
         copy.wait()
 
     def spot(j, s):
@@ -409,28 +419,30 @@
             gap = SIGMA * (tile(nv, 1, j, s) - tile(nv, 0, j, s))
             di[(0,) + spot(j, s)] = clip(gap, tile(bv, 0, j, s))
 
-    def body(p, total):
-        @pl.when((p + 1) % CHUNK == 0)
+    def body(step, total):
+        @pl.when(step > 0)
         def _():
-            for copy in reads((p + 1) // CHUNK):
+            for copy in reads(step, step * GROUP + 2, GROUP):
                 copy.wait()
 
-        for s in range(4):
-            n = [tile(nv, p, j, s) for j in range(depth)]
-            b = [tile(bv, p, j, s) for j in range(depth)]
-            c = [-k for k in b]
-            z = [clip2(SIGMA * (m - o), k, l) for m, o, k, l in zip(depth_next(n), n, b, c)]
-            back = depth_back(z)
-            for j in range(depth):
-                new = clip2(SIGMA * (tile(nv, p + 1, j, s) - n[j]), b[j], c[j])
-                at = (p,) + spot(j, s)
-                di[at] = new
-                dz[at] = z[j]
-                part[at] = (new - tile(di, p - 1, j, s)) + (z[j] - back[j])
-                total = total + (new * new + z[j] * z[j])
+        for k in range(GROUP):
+            p = step * GROUP + 1 + k
+            for s in range(4):
+                n = [tile(nv, p, j, s) for j in range(depth)]
+                b = [tile(bv, p, j, s) for j in range(depth)]
+                c = [-k for k in b]
+                z = [clip2(SIGMA * (m - o), k, l) for m, o, k, l in zip(depth_next(n), n, b, c)]
+                back = depth_back(z)
+                for j in range(depth):
+                    new = clip2(SIGMA * (tile(nv, p + 1, j, s) - n[j]), b[j], c[j])
+                    at = (p,) + spot(j, s)
+                    di[at] = new
+                    dz[at] = z[j]
+                    part[at] = (new - tile(di, p - 1, j, s)) + (z[j] - back[j])
+                    total = total + (new * new + z[j] * z[j])
         return total
 
-    sum_ref[...] = lax.fori_loop(1, ni - 1, body, jnp.zeros((8, LANES), F32))
+    sum_ref[0] = lax.fori_loop(0, steps, body, jnp.zeros((8, LANES), F32))
 
 
 def own(noisy, bound):
@@ -438,21 +450,21 @@
     whole = pltpu.VMEM((ni, nx, nz), F32)
     return pl.pallas_call(
         own_kernel,
-        out_shape=(whole,) * 5 + (pltpu.VMEM((8, LANES), F32),),
+        out_shape=(whole,) * 5 + (pltpu.VMEM((4, 8, LANES), F32),),
         in_specs=[pl.BlockSpec(memory_space=HBM)] * 2,
         out_specs=[pl.BlockSpec(memory_space=VMEM)] * 6,
-        scratch_shapes=[pltpu.SemaphoreType.DMA((2, ni // CHUNK))],
+        scratch_shapes=[pltpu.SemaphoreType.DMA((2, (ni - 2) // GROUP))],
         compiler_params=pltpu.CompilerParams(vmem_limit_bytes=16 << 20),
         cost_estimate=pl.CostEstimate(flops=100_000_000, transcendentals=0, bytes_accessed=4 << 20),
         name="own_planes",
     )(noisy, bound)
 
 
-def inner_kernel(flags, nv, bv, di, dz, part, own_sum, hn, hb, u_hbm, d_hbm, sums_ref, *refs):
+def inner_kernel(nv, bv, di, dz, part, own_sum, hn, hb, u_hbm, d_hbm, sums_ref, *refs):
     handed, refs = refs[: len(HANDED)], refs[len(HANDED) :]
     ve, ue, dh, dx, div1, dx2, di2, uo, do, u_sems, d_sems = refs
     ni, depth = nv.shape[0], nv.shape[2] // LANES
-    more_x = flags[1] > 0
+    more_x = place()[1]
     parts = (ni - 4) // PART
 
     def bound_of(p, j, s):
@@ -557,27 +569,25 @@
     for j, value in enumerate(halo_i(0)):
         dh[0, j, 0:8, :] = value
     zero = jnp.zeros((8, LANES), F32)
-    a = first_inner(1, (zero, own_sum[...]))
+    a = first_inner(1, (zero, own_sum[0]))
     a = first_inner(2, a)
     for s in range(4):
         for j in range(depth):
             second_i(t, 1, s, j)
     hand((1, 2, 3))
 
-    def body(p, carry):
+    def body(step, carry):
         a, b = carry
-        ready(p + 1)
-        a = first_inner(p, a)
-        b = second(t, p - 1, p - 1, depth, b, uo, do)
-
-        @pl.when(p % PART == 0)
-        def _():
-            for copy in writes(p // PART - 2):
-                copy.start()
-
+        for k in range(PART):
+            p = step * PART + 3 + k
+            ready(p + 1)
+            a = first_inner(p, a)
+            b = second(t, p - 1, p - 1, depth, b, uo, do)
+        for copy in writes(step):
+            copy.start()
         return a, b
 
-    a, b = lax.fori_loop(3, ni - 1, body, (a, (zero, zero)))
+    a, b = lax.fori_loop(0, parts, body, (a, (zero, zero)))
     hand((4, 5, 6))
     for k, total in enumerate(a + b):
         sums_ref[k] = total
@@ -586,7 +596,7 @@
             copy.wait()
 
 
-def inner(flags, nv, bv, di, dz, part, own_sum, halo_n, halo_b):
+def inner(nv, bv, di, dz, part, own_sum, halo_n, halo_b):
     ni, nx, nz = nv.shape
     depth = nz // LANES
     full = pltpu.VMEM((ni, depth, ROWS, LANES), F32)
@@ -601,7 +611,7 @@
             pltpu.VMEM((4, 8, LANES), F32),
         )
         + (slots,) * len(HANDED),
-        in_specs=[pl.BlockSpec(memory_space=pltpu.SMEM)] + [pl.BlockSpec(memory_space=VMEM)] * 8,
+        in_specs=[pl.BlockSpec(memory_space=VMEM)] * 8,
         out_specs=[pl.BlockSpec(memory_space=HBM)] * 2
         + [pl.BlockSpec(memory_space=VMEM)] * (1 + len(HANDED)),
         scratch_shapes=[full] * 2
@@ -616,17 +626,17 @@
         compiler_params=pltpu.CompilerParams(vmem_limit_bytes=24 << 20),
         cost_estimate=pl.CostEstimate(flops=200_000_000, transcendentals=0, bytes_accessed=12 << 20),
         name="inner_planes",
-    )(flags, nv, bv, di, dz, part, own_sum, halo_n, halo_b)
-
-
-def edge_kernel(flags, got_a, got_c, n4_ref, b4_ref, hb, sums_ref, *refs):
+    )(nv, bv, di, dz, part, own_sum, halo_n, halo_b)
+
+
+def edge_kernel(got_a, got_c, n4_ref, b4_ref, hb, sums_ref, *refs):
     given = dict(zip([name for name, _ in HANDED], refs))
     refs = refs[len(HANDED) :]
     _, _, u_hbm, d_hbm, spread_ref = refs[:5]
     ve, ue, di, dx, dz, div1, di2, dx2, uo, do, u_sems, d_sems = refs[5:]
     own = dict(ve=ve, ue=ue, di=di, dx=dx, dz=dz, div1=div1, di2=di2)
     depth, ni = got_a.shape[0], u_hbm.shape[0]
-    more_i, more_x, even_i = flags[0] > 0, flags[1] > 0, flags[2] == 0
+    more_i, more_x, even_i, _ = place()
 
     def up(j, row):
         rows = pl.ds(row, 8)
@@ -703,11 +713,11 @@
         copy.wait()
 
 
-def edges(flags, got_a, got_c, n4, b4, halo_b, sums, handed, primal, dual, devices):
+def edges(got_a, got_c, n4, b4, halo_b, sums, handed, primal, dual, devices):
     _, nx, nz = primal.shape
     depth = nz // LANES
     buffer = pltpu.VMEM((8, depth, ROWS, LANES), F32)
-    count = 7 + len(handed)
+    count = 6 + len(handed)
     return pl.pallas_call(
         edge_kernel,
         out_shape=(
@@ -715,8 +725,7 @@
             jax.ShapeDtypeStruct(dual.shape, F32),
             jax.ShapeDtypeStruct((devices, 4), F32),
         ),
-        in_specs=[pl.BlockSpec(memory_space=pltpu.SMEM)]
-        + [pl.BlockSpec(memory_space=VMEM)] * (count - 1)
+        in_specs=[pl.BlockSpec(memory_space=VMEM)] * count
         + [pl.BlockSpec(memory_space=HBM)] * 2,
         out_specs=[pl.BlockSpec(memory_space=HBM)] * 2 + [pl.BlockSpec(memory_space=VMEM)],
         scratch_shapes=[buffer] * 8
@@ -729,33 +738,24 @@
         input_output_aliases={count: 0, count + 1: 1},
         compiler_params=pltpu.CompilerParams(vmem_limit_bytes=24 << 20),
         name="edge_planes",
-    )(flags, got_a, got_c, n4, b4, halo_b, sums, *handed, primal, dual)
+    )(got_a, got_c, n4, b4, halo_b, sums, *handed, primal, dual)
 
 
 def per_device(noisy, bound):
     count_i, count_x = lax.axis_size("inl"), lax.axis_size("xln")
-    at_i, at_x = lax.axis_index("inl"), lax.axis_index("xln")
-    flags = jnp.stack(
-        [
-            (at_i < count_i - 1).astype(jnp.int32),
-            (at_x < count_x - 1).astype(jnp.int32),
-            at_i % 2,
-            at_x % 2,
-        ]
-    )
     noisy, bound = (pltpu.with_memory_space_constraint(x, HBM) for x in (noisy, bound))
-    send_a, send_c, n4, b4 = pack(flags, noisy, bound)
+    send_a, send_c, n4, b4 = pack(noisy, bound)
     got_c = swapped(send_c, "xln", 1)
     got_a = swapped(send_a, "xln", 0)
     alone = own(noisy, bound)
     face_a, face_c, halo_n, halo_b = planes(
-        flags, n4, b4, send_a, send_c, got_a, got_c, alone[-1]
+        n4, b4, send_a, send_c, got_a, got_c, alone[-1]
     )
     back_a = swapped(face_a, "inl", 0)
     back_c = swapped(face_c, "inl", 1)
-    primal, dual, sums, *handed = inner(flags, *alone, halo_n, halo_b)
+    primal, dual, sums, *handed = inner(*alone, halo_n, halo_b)
     primal, dual, spread = edges(
-        flags, back_a, back_c, n4, b4, halo_b, sums, handed, primal, dual, count_i * count_x
+        back_a, back_c, n4, b4, halo_b, sums, handed, primal, dual, count_i * count_x
     )
     parts = lax.all_to_all(spread, AXES, 0, 0, tiled=True)
     norms = jnp.sqrt(jnp.sum(parts, axis=0)).reshape(2, 2)

time: 59.9 us -> 53.4 us (0.89)
  Pallas kernels: 23.1 us -> 12.9 us
  waiting for transfers between devices: 0.01 us -> 2.78 us
  blocking collectives: 27.9 us -> 30 us
  starting transfers between devices: 6.98 us -> 5.96 us
    pallas_call x1, Pallas kernels: 11.5 us -> 6.06 us  [inner(): pl.pallas_call(inner_kernel, out_shape=(jax.ShapeDtypeStruct((ni, nx, nz)...]
    pallas_call x1, Pallas kernels: 6.31 us -> 3.27 us  [own(): pl.pallas_call(own_kernel, out_shape=(whole,) * 5 + (pltpu.VMEM((4, 8, LA...]
    ppermute x4, waiting for transfers between devices: 0.01 us -> 2.78 us  [swapped(): return lax.ppermute(value, axis, pairs)]
    all_to_all x1, blocking collectives: 27.9 us -> 30 us  [per_device(): parts = lax.all_to_all(spread, AXES, 0, 0, tiled=True)]
    ppermute x4, starting transfers between devices: 6.98 us -> 5.96 us  [swapped(): return lax.ppermute(value, axis, pairs)]
    pallas_call x1, Pallas kernels: 2.18 us -> 1.54 us  [edges(): pl.pallas_call(edge_kernel, out_shape=(jax.ShapeDtypeStruct(primal.shape,...]
  transfers between devices with their start and end apart: 4 -> 4, of which waited for: 0 -> 1; matrix products, arithmetic and copies ran while one was open for 0% -> 0% of each run, Pallas kernels for 30% -> 18%
where the time goes in v4:
time: 53.4 us; the launch traced here: 53.3 us
  blocking collectives  30 us (56%)
  Pallas kernels  12.9 us (24%)
  starting transfers between devices  5.96 us (11%)
  waiting for transfers between devices  2.78 us (5%)
  between operations  0.72 us (1%)
  local copies, waits for them, and re-layouts  0.66 us (1%)
    all_to_all x1, blocking collectives, per_device(): parts = lax.all_to_all(spread, AXES, 0, 0, tiled=True)  30 us
    pallas_call x1, Pallas kernels, inner(): pl.pallas_call(inner_kernel, out_shape=(jax.ShapeDtypeStruct((ni, nx, nz)...  6.06 us
    ppermute x4, starting transfers between devices, swapped(): return lax.ppermute(value, axis, pairs)  5.96 us
    pallas_call x1, Pallas kernels, own(): pl.pallas_call(own_kernel, out_shape=(whole,) * 5 + (pltpu.VMEM((4, 8, LA...  3.27 us
    ppermute x4, waiting for transfers between devices, swapped(): return lax.ppermute(value, axis, pairs)  2.78 us
    pallas_call x1, Pallas kernels, edges(): pl.pallas_call(edge_kernel, out_shape=(jax.ShapeDtypeStruct(primal.shape,...  1.54 us
    pallas_call x1, Pallas kernels, pack(): pl.pallas_call(pack_kernel, out_shape=(message, message, boundary, bounda...  1.45 us
  transfers between devices with their start and end apart: 4, of which 1 were waited for; matrix products, arithmetic and copies ran while one was open for 0% of the time, Pallas kernels for 18%

profile of v4, /device:TPU:1, one launch (start us, length us, event | category | flops | bytes accessed | tf_op | source)
XLA Modules:
  0.0 53.3 jit_solution(13699753770991804316)
XLA Ops:
  0.6 1.4 %pack_faces.1 = (f32[32,4,4,128]{3,2,1,0:T(4,128)S(1)}, f32[32,4,4,128]{3,2,1,0:T(4,128)S(1)}, f32[4,32,512]{2,1,0:T(8,128)S(1)}, f32[4,32,512]{2,1,0:T(8,128)S(1)}) custom-call(f32[32,32,512]{2,1,0:T(8,128)} %n_hbm.3, f32[32,32,512]{2,1,0:T(8,128)} %b_hbm.3), custom_call_target="tpu_custom_call" | custom-call | tf_op jit(solution)/shard_map/pack_faces/pallas_call | solution.py:105
  2.1 3.3 %collective-permute-start = (f32[32,4,4,128]{3,2,1,0:T(4,128)S(1)}, f32[32,4,4,128]{3,2,1,0:T(4,128)S(1)}, u32[]{:S(2)}, u32[]{:S(2)}) collective-permute-start(f32[32,4,4,128]{3,2,1,0:T(4,128)S(1)} %get-tuple-element.32.sent_a), channel_id=1, source_target_pairs={{0,1},{1,0},{2,3},{3,2},{4,5},{5,4},{6,7},{7,6},{8,9},{9,8},{10,11... | collective-permute-start | bytes 786440 | tf_op jit(solution)/shard_map/ppermute | solution.py:27
  5.4 1.9 %collective-permute-start.1 = (f32[32,4,4,128]{3,2,1,0:T(4,128)S(1)}, f32[32,4,4,128]{3,2,1,0:T(4,128)S(1)}, u32[]{:S(2)}, u32[]{:S(2)}) collective-permute-start(f32[32,4,4,128]{3,2,1,0:T(4,128)S(1)} %get-tuple-element.33.sent_c), channel_id=1, source_target_pairs={{1,2},{2,1},{3,4},{4,3},{5,6},{6,5},{7,8},{8,7},{9,10},{10,9},{11,... | collective-permute-start | bytes 786440 | tf_op jit(solution)/shard_map/ppermute | solution.py:27
  7.3 3.3 %own_planes.1 = (f32[32,32,512]{2,1,0:T(8,128)S(1)}, f32[32,32,512]{2,1,0:T(8,128)S(1)}, f32[32,32,512]{2,1,0:T(8,128)S(1)}, f32[32,32,512]{2,1,0:T(8,128)S(1)},...) custom-call(f32[32,32,512]{2,1,0:T(8,128)} %n_hbm.3, f32[32,32,512]{2,1,0:T(8,128)} %b_hbm.3), custom_call_target="tpu_custom_call" | custom-call | flops 100000000 | bytes 4194304 | tf_op jit(solution)/shard_map/own_planes/pallas_call | solution.py:451
  10.6 0.0 collective-permute-done.got_a
  10.6 2.8 %collective-permute-done.1.got_c = f32[32,4,4,128]{3,2,1,0:T(4,128)S(1)} collective-permute-done((f32[32,4,4,128]{3,2,1,0:T(4,128)S(1)}, f32[32,4,4,128]{3,2,1,0:T(4,128)S(1)}, u32[]{:S(2)}, u32[]{:S(2)}) %collective-permute-start.1) | collective-permute-done | bytes 262176 | tf_op jit(solution)/shard_map/ppermute | solution.py:27
  13.3 0.5 %pack_planes.1 = (f32[4,112,128]{2,1,0:T(8,128)S(1)}, f32[4,112,128]{2,1,0:T(8,128)S(1)}, f32[32,4,8,128]{3,2,1,0:T(8,128)S(1)}, f32[32,4,8,128]{3,2,1,0:T(8,128)S(1)}) custom-call(f32[4,32,512]{2,1,0:T(8,128)S(1)} %get-tuple-element.30.n4_ref, f32[4,32,512]{2,1,0:T(8,128)S(1)} %get-tuple-element.31.b4_ref, f32[32,4,4,128]{3,2,1,0:T(4,128)S(1)} %get-tuple-element.32.sent_a, ...), custom_call_target="tpu_custom_call" | custom-call | tf_op jit(solution)/shard_map/pack_planes/pallas_call | solution.py:265
  13.9 0.1 collective-permute-start.2
  14.0 0.7 %collective-permute-start.3 = (f32[4,112,128]{2,1,0:T(8,128)S(1)}, f32[4,112,128]{2,1,0:T(8,128)S(1)}, u32[]{:S(2)}, u32[]{:S(2)}) collective-permute-start(f32[4,112,128]{2,1,0:T(8,128)S(1)} %get-tuple-element.36), channel_id=1, source_target_pairs={{32,64},{64,32},{96,128},{128,96},{160,192},{192,160},{33,65},{65,... | collective-permute-start | bytes 688136 | tf_op jit(solution)/shard_map/ppermute | solution.py:27
  14.7 6.1 %inner_planes.1 = (f32[32,32,512]{2,1,0:T(8,128)}, f32[3,32,32,512]{3,2,1,0:T(8,128)}, f32[4,8,128]{2,1,0:T(8,128)S(1)}, f32[8,4,56,128]{3,2,1,0:T(8,128)S(1)}, ...) custom-call(f32[32,32,512]{2,1,0:T(8,128)S(1)} %get-tuple-element.38, ...), custom_call_target="tpu_custom_call" | custom-call | flops 200000000 | bytes 12582912 | tf_op jit(solution)/shard_map/inner_planes/pallas_call | solution.py:606
  20.7 0.0 collective-permute-done.2.got_a
  20.8 0.0 collective-permute-done.3.got_c
  20.8 1.5 %edge_planes.1 = (f32[32,32,512]{2,1,0:T(8,128)}, f32[3,32,32,512]{3,2,1,0:T(8,128)}, f32[256,4]{1,0:T(8,128)S(1)}) custom-call(f32[4,112,128]{2,1,0:T(8,128)S(1)} %collective-permute-done.2.got_a, f32[4,112,128]{2,1,0:T(8,128)S(1)} %collective-permute-done.3.got_c, ...), custom_call_target="tpu_custom_call", output_to_operand_aliasing={{0}: (13, {}), {1}: (14, {})} | custom-call | tf_op jit(solution)/shard_map/edge_planes/pallas_call | solution.py:721
  22.3 30.0 %all_to_all.9 = f32[256,1,4]{2,1,0:T(1,128)S(1)} all-to-all(f32[256,1,4]{2,1,0:T(1,128)S(1)} %bitcast.3), channel_id=1, replica_groups=mesh['inl'=8,'xln'=32] {'inl','xln'}, dimensions={0} | all-to-all | bytes 8192 | tf_op jit(solution)/shard_map/all_to_all | solution.py:760
  52.3 0.3 reduce_sum.9
  52.6 0.7 %sqrt.8 = f32[2,2]{1,0:T(2,128)} reshape(f32[4]{0:T(128)S(1)} %sqrt.7) | data formatting | bytes 32 | tf_op jit(solution)/shard_map/sqrt | solution.py:761
  (1 shorter events, 0.0 us)
Async XLA Ops:
  2.1 8.5 %collective-permute-start = (f32[32,4,4,128]{3,2,1,0:T(4,128)S(1)}, f32[32,4,4,128]{3,2,1,0:T(4,128)S(1)}, u32[]{:S(2)}, u32[]{:S(2)}) collective-permute-start(f32[32,4,4,128]{3,2,1,0:T(4,128)S(1)} %get-tuple-element.32.sent_a), channel_id=1, source_target_pairs={{0,1},{1,0},{2,3},{3,2},{4,5},{5,4},{6,7},{7,6},{8,9},{9,8},{10,11... | collective-permute-start | bytes 786440 | tf_op jit(solution)/shard_map/ppermute | solution.py:27
  5.4 8.0 %collective-permute-start.1 = (f32[32,4,4,128]{3,2,1,0:T(4,128)S(1)}, f32[32,4,4,128]{3,2,1,0:T(4,128)S(1)}, u32[]{:S(2)}, u32[]{:S(2)}) collective-permute-start(f32[32,4,4,128]{3,2,1,0:T(4,128)S(1)} %get-tuple-element.33.sent_c), channel_id=1, source_target_pairs={{1,2},{2,1},{3,4},{4,3},{5,6},{6,5},{7,8},{8,7},{9,10},{10,9},{11,... | collective-permute-start | bytes 786440 | tf_op jit(solution)/shard_map/ppermute | solution.py:27
  13.9 6.9 %collective-permute-start.2 = (f32[4,112,128]{2,1,0:T(8,128)S(1)}, f32[4,112,128]{2,1,0:T(8,128)S(1)}, u32[]{:S(2)}, u32[]{:S(2)}) collective-permute-start(f32[4,112,128]{2,1,0:T(8,128)S(1)} %get-tuple-element.35), channel_id=1, source_target_pairs={{0,32},{32,0},{64,96},{96,64},{128,160},{160,128},{192,224},{224,1... | collective-permute-start | bytes 688136 | tf_op jit(solution)/shard_map/ppermute | solution.py:27
  14.0 6.8 %collective-permute-start.3 = (f32[4,112,128]{2,1,0:T(8,128)S(1)}, f32[4,112,128]{2,1,0:T(8,128)S(1)}, u32[]{:S(2)}, u32[]{:S(2)}) collective-permute-start(f32[4,112,128]{2,1,0:T(8,128)S(1)} %get-tuple-element.36), channel_id=1, source_target_pairs={{32,64},{64,32},{96,128},{128,96},{160,192},{192,160},{33,65},{65,... | collective-permute-start | bytes 688136 | tf_op jit(solution)/shard_map/ppermute | solution.py:27

commit v5 on v4

--- a/solution.py
+++ b/solution.py
@@ -5,11 +5,13 @@
 from jax.experimental.pallas import tpu as pltpu
 from jax.sharding import PartitionSpec as P
 
+
 SIGMA = 0.28
 TAU = 0.28
 C = TAU / (1.0 + TAU)
 C_OLD = C / (1.0 + TAU)
 TWO_CS = 2.0 * C * SIGMA
+WIDE = 1e30
 
 LANES = 128
 ROWS = 56
@@ -63,9 +65,9 @@
     even = place()[3]
     columns, planes = [], []
     for k, src in enumerate((n_hbm, b_hbm)):
-        for m, start in enumerate((nx - 2, 0)):
+        for m, x in enumerate((nx - 2, nx - 1, 0, 1)):
             columns.append(
-                pltpu.make_async_copy(src.at[:, pl.ds(start, 2), :], slab.at[m, k], sems.at[m, k])
+                pltpu.make_async_copy(src.at[:, x, :], slab.at[m, k], sems.at[m, k])
             )
     for k, (src, dst) in enumerate(((n_hbm, n4_ref), (b_hbm, b4_ref))):
         for q, i in enumerate((0, ni - 2)):
@@ -79,16 +81,15 @@
     for c in columns:
         c.wait()
 
-    def body(i, _):
-        for k in range(2):
-            for j in range(depth):
-                lanes = pl.ds(j * LANES, LANES)
-                high, low = slab[0, k, i, 0:2, lanes], slab[1, k, i, 0:2, lanes]
-                a_ref[i, j, 2 * k : 2 * k + 2, :] = jnp.where(even, high, low)
-                c_ref[i, j, 2 * k : 2 * k + 2, :] = jnp.where(even, low, high)
-        return 0
-
-    lax.fori_loop(0, ni, body, 0, unroll=2)
+    for r in range(0, ni, 8):
+        rows = pl.ds(r, 8)
+        n = [slab[m, 0, rows, :] for m in range(4)]
+        b = [slab[m, 1, rows, :] for m in range(3)]
+        high = n[1], b[1], clip(SIGMA * (n[1] - n[0]), b[0])
+        low = n[2], b[2], clip(SIGMA * (n[3] - n[2]), b[2])
+        for k, (h, l) in enumerate(zip(high, low)):
+            a_ref[k, rows, :] = jnp.where(even, h, l)
+            c_ref[k, rows, :] = jnp.where(even, l, h)
     for c in planes:
         c.wait()
 
@@ -100,7 +101,7 @@
 def pack(noisy, bound):
     ni, nx, nz = noisy.shape
     depth = nz // LANES
-    message = pltpu.VMEM((ni, depth, 4, LANES), F32)
+    message = pltpu.VMEM((3, ni, nz), F32)
     boundary = pltpu.VMEM((4, nx, nz), F32)
     return pl.pallas_call(
         pack_kernel,
@@ -108,8 +109,8 @@
         in_specs=[pl.BlockSpec(memory_space=HBM)] * 2,
         out_specs=[pl.BlockSpec(memory_space=VMEM)] * 4,
         scratch_shapes=[
-            pltpu.VMEM((2, 2, ni, 2, nz), F32),
-            pltpu.SemaphoreType.DMA((2, 2)),
+            pltpu.VMEM((4, 2, ni, nz), F32),
+            pltpu.SemaphoreType.DMA((4, 2)),
             pltpu.SemaphoreType.DMA((2, 2)),
         ],
         compiler_params=pltpu.CompilerParams(vmem_limit_bytes=8 << 20),
@@ -189,25 +190,35 @@
 
 def planes_kernel(
     n4_ref, b4_ref, sent_a, sent_c, got_a, got_c, _,
-    a_ref, c_ref, hn, hb, ve, dx,
+    a_ref, c_ref, hn, hb, ve, dx, far,
 ):
-    ni, depth = got_a.shape[0], got_a.shape[1]
+    ni, depth = got_a.shape[1], got_a.shape[2] // LANES
     _, more_x, even_i, even_x = place()
 
-    def sort(i, _):
-        for j in range(depth):
-            last = jnp.where(even_x, sent_a[i, j, 1:2, :], sent_c[i, j, 1:2, :])
-            a_n, c_n = got_a[i, j, 0:2, :], got_c[i, j, 0:2, :]
-            a_b, c_b = got_a[i, j, 2:4, :], got_c[i, j, 2:4, :]
-            hn[i, j, 6:8, :] = jnp.where(even_x, c_n, a_n)
-            hb[i, j, 6:8, :] = jnp.where(even_x, c_b, a_b)
-            above = jnp.where(even_x, a_n, c_n)
-            hn[i, j, 0:2, :] = above
-            hb[i, j, 0:2, :] = jnp.where(even_x, a_b, c_b)
-            hn[i, j, 0:1, :] = jnp.where(more_x, above[0:1], last)
-        return 0
-
-    lax.fori_loop(0, ni, sort, 0, unroll=2)
+    for r in range(0, ni, 8):
+        rows = pl.ds(r, 8)
+        a = [got_a[k, rows, :] for k in range(3)]
+        c = [got_c[k, rows, :] for k in range(3)]
+        after = [jnp.where(even_x, k, m) for k, m in zip(a, c)]
+        before = [jnp.where(even_x, m, k) for k, m in zip(a, c)]
+        last = jnp.where(even_x, sent_a[0, rows, :], sent_c[0, rows, :])
+        far[0, rows, :] = jnp.where(more_x, after[0], last)
+        far[1, rows, :] = after[0] + after[2] * (1.0 / SIGMA)
+        far[2, rows, :] = before[0] - before[2] * (1.0 / SIGMA)
+        far[3, rows, :] = before[0]
+        far[4, rows, :] = after[1]
+        far[5, rows, :] = before[1]
+
+    wide = jnp.full((1, LANES), WIDE, F32)
+
+    for i in range(ni):
+        for j in range(depth):
+            lanes = pl.ds(j * LANES, LANES)
+            for k, row in enumerate((0, 1, 6, 7)):
+                hn[i, j, row : row + 1, :] = far[k, i : i + 1, lanes]
+            hb[i, j, 0:1, :] = far[4, i : i + 1, lanes]
+            hb[i, j, 6:7, :] = wide
+            hb[i, j, 7:8, :] = far[5, i : i + 1, lanes]
     planes_at = (0, 1, ni - 2, ni - 1)
 
     def image_of(q, j, s):
@@ -260,7 +271,7 @@
 
 
 def planes(n4, b4, sent_a, sent_c, got_a, got_c, after):
-    ni, depth = got_a.shape[0], got_a.shape[1]
+    ni, depth = got_a.shape[1], got_a.shape[2] // LANES
     buffer = pltpu.VMEM((4, depth, ROWS, LANES), F32)
     return pl.pallas_call(
         planes_kernel,
@@ -268,7 +279,7 @@
         + (pltpu.VMEM((ni, depth, 8, LANES), F32),) * 2,
         in_specs=[pl.BlockSpec(memory_space=VMEM)] * 7,
         out_specs=[pl.BlockSpec(memory_space=VMEM)] * 4,
-        scratch_shapes=[buffer] * 2,
+        scratch_shapes=[buffer] * 2 + [pltpu.VMEM((6, ni, depth * LANES), F32)],
         compiler_params=pltpu.CompilerParams(vmem_limit_bytes=8 << 20),
         name="pack_planes",
     )(n4, b4, sent_a, sent_c, got_a, got_c, after)

time: 53.4 us -> 52.8 us (0.989)
  waiting for transfers between devices: 2.78 us -> 1.78 us
    ppermute x4, waiting for transfers between devices: 2.78 us -> 1.78 us  [swapped(): return lax.ppermute(value, axis, pairs)]
where the time goes in v5:
time: 52.8 us; the launch traced here: 52.6 us
  blocking collectives  30.3 us (57%)
  Pallas kernels  12.9 us (24%)
  starting transfers between devices  5.96 us (11%)
  waiting for transfers between devices  1.78 us (3%)
  between operations  0.72 us (1%)
  local copies, waits for them, and re-layouts  0.66 us (1%)
    all_to_all x1, blocking collectives, per_device(): parts = lax.all_to_all(spread, AXES, 0, 0, tiled=True)  30.3 us
    pallas_call x1, Pallas kernels, inner(): pl.pallas_call(inner_kernel, out_shape=(jax.ShapeDtypeStruct((ni, nx, nz)...  6.06 us
    ppermute x4, starting transfers between devices, swapped(): return lax.ppermute(value, axis, pairs)  5.96 us
    pallas_call x1, Pallas kernels, own(): pl.pallas_call(own_kernel, out_shape=(whole,) * 5 + (pltpu.VMEM((4, 8, LA...  3.27 us
    ppermute x4, waiting for transfers between devices, swapped(): return lax.ppermute(value, axis, pairs)  1.78 us
    pallas_call x1, Pallas kernels, edges(): pl.pallas_call(edge_kernel, out_shape=(jax.ShapeDtypeStruct(primal.shape,...  1.54 us
    pallas_call x1, Pallas kernels, pack(): pl.pallas_call(pack_kernel, out_shape=(message, message, boundary, bounda...  1.47 us
  transfers between devices with their start and end apart: 4, of which 1 were waited for; matrix products, arithmetic and copies ran while one was open for 0% of the time, Pallas kernels for 18%

profile of v5, /device:TPU:1, one launch (start us, length us, event | category | flops | bytes accessed | tf_op | source)
XLA Modules:
  0.0 52.6 jit_solution(18433315021069750449)
XLA Ops:
  0.6 1.5 %pack_faces.1 = (f32[3,32,512]{2,1,0:T(8,128)S(1)}, f32[3,32,512]{2,1,0:T(8,128)S(1)}, f32[4,32,512]{2,1,0:T(8,128)S(1)}, f32[4,32,512]{2,1,0:T(8,128)S(1)}) custom-call(f32[32,32,512]{2,1,0:T(8,128)} %n_hbm.3, f32[32,32,512]{2,1,0:T(8,128)} %b_hbm.3), custom_call_target="tpu_custom_call" | custom-call | tf_op jit(solution)/shard_map/pack_faces/pallas_call | solution.py:106
  2.1 3.3 %collective-permute-start = (f32[3,32,512]{2,1,0:T(8,128)S(1)}, f32[3,32,512]{2,1,0:T(8,128)S(1)}, u32[]{:S(2)}, u32[]{:S(2)}) collective-permute-start(f32[3,32,512]{2,1,0:T(8,128)S(1)} %get-tuple-element.32.sent_a), channel_id=1, source_target_pairs={{0,1},{1,0},{2,3},{3,2},{4,5},{5,4},{6,7},{7,6},{8,9},{9,8},{10,11... | collective-permute-start | bytes 589832 | tf_op jit(solution)/shard_map/ppermute | solution.py:29
  5.4 1.9 %collective-permute-start.1 = (f32[3,32,512]{2,1,0:T(8,128)S(1)}, f32[3,32,512]{2,1,0:T(8,128)S(1)}, u32[]{:S(2)}, u32[]{:S(2)}) collective-permute-start(f32[3,32,512]{2,1,0:T(8,128)S(1)} %get-tuple-element.33.sent_c), channel_id=1, source_target_pairs={{1,2},{2,1},{3,4},{4,3},{5,6},{6,5},{7,8},{8,7},{9,10},{10,9},{11,... | collective-permute-start | bytes 589832 | tf_op jit(solution)/shard_map/ppermute | solution.py:29
  7.3 3.3 %own_planes.1 = (f32[32,32,512]{2,1,0:T(8,128)S(1)}, f32[32,32,512]{2,1,0:T(8,128)S(1)}, f32[32,32,512]{2,1,0:T(8,128)S(1)}, f32[32,32,512]{2,1,0:T(8,128)S(1)},...) custom-call(f32[32,32,512]{2,1,0:T(8,128)} %n_hbm.3, f32[32,32,512]{2,1,0:T(8,128)} %b_hbm.3), custom_call_target="tpu_custom_call" | custom-call | flops 100000000 | bytes 4194304 | tf_op jit(solution)/shard_map/own_planes/pallas_call | solution.py:462
  10.6 0.0 collective-permute-done.got_a
  10.6 1.8 %collective-permute-done.1.got_c = f32[3,32,512]{2,1,0:T(8,128)S(1)} collective-permute-done((f32[3,32,512]{2,1,0:T(8,128)S(1)}, f32[3,32,512]{2,1,0:T(8,128)S(1)}, u32[]{:S(2)}, u32[]{:S(2)}) %collective-permute-start.1) | collective-permute-done | bytes 196640 | tf_op jit(solution)/shard_map/ppermute | solution.py:29
  12.4 0.5 %pack_planes.1 = (f32[4,112,128]{2,1,0:T(8,128)S(1)}, f32[4,112,128]{2,1,0:T(8,128)S(1)}, f32[32,4,8,128]{3,2,1,0:T(8,128)S(1)}, f32[32,4,8,128]{3,2,1,0:T(8,128)S(1)}) custom-call(f32[4,32,512]{2,1,0:T(8,128)S(1)} %get-tuple-element.30.n4_ref, f32[4,32,512]{2,1,0:T(8,128)S(1)} %get-tuple-element.31.b4_ref, f32[3,32,512]{2,1,0:T(8,128)S(1)} %get-tuple-element.32.sent_a, ...), custom_call_target="tpu_custom_call" | custom-call | tf_op jit(solution)/shard_map/pack_planes/pallas_call | solution.py:276
  12.9 0.1 collective-permute-start.2
  13.0 0.7 %collective-permute-start.3 = (f32[4,112,128]{2,1,0:T(8,128)S(1)}, f32[4,112,128]{2,1,0:T(8,128)S(1)}, u32[]{:S(2)}, u32[]{:S(2)}) collective-permute-start(f32[4,112,128]{2,1,0:T(8,128)S(1)} %get-tuple-element.36), channel_id=1, source_target_pairs={{32,64},{64,32},{96,128},{128,96},{160,192},{192,160},{33,65},{65,... | collective-permute-start | bytes 688136 | tf_op jit(solution)/shard_map/ppermute | solution.py:29
  13.7 6.1 %inner_planes.1 = (f32[32,32,512]{2,1,0:T(8,128)}, f32[3,32,32,512]{3,2,1,0:T(8,128)}, f32[4,8,128]{2,1,0:T(8,128)S(1)}, f32[8,4,56,128]{3,2,1,0:T(8,128)S(1)}, ...) custom-call(f32[32,32,512]{2,1,0:T(8,128)S(1)} %get-tuple-element.38, ...), custom_call_target="tpu_custom_call" | custom-call | flops 200000000 | bytes 12582912 | tf_op jit(solution)/shard_map/inner_planes/pallas_call | solution.py:617
  19.8 0.0 collective-permute-done.2.got_a
  19.8 0.0 collective-permute-done.3.got_c
  19.8 1.5 %edge_planes.1 = (f32[32,32,512]{2,1,0:T(8,128)}, f32[3,32,32,512]{3,2,1,0:T(8,128)}, f32[256,4]{1,0:T(8,128)S(1)}) custom-call(f32[4,112,128]{2,1,0:T(8,128)S(1)} %collective-permute-done.2.got_a, f32[4,112,128]{2,1,0:T(8,128)S(1)} %collective-permute-done.3.got_c, ...), custom_call_target="tpu_custom_call", output_to_operand_aliasing={{0}: (13, {}), {1}: (14, {})} | custom-call | tf_op jit(solution)/shard_map/edge_planes/pallas_call | solution.py:732
  21.4 30.3 %all_to_all.9 = f32[256,1,4]{2,1,0:T(1,128)S(1)} all-to-all(f32[256,1,4]{2,1,0:T(1,128)S(1)} %bitcast.3), channel_id=1, replica_groups=mesh['inl'=8,'xln'=32] {'inl','xln'}, dimensions={0} | all-to-all | bytes 8192 | tf_op jit(solution)/shard_map/all_to_all | solution.py:771
  51.7 0.3 reduce_sum.9
  52.0 0.7 %sqrt.8 = f32[2,2]{1,0:T(2,128)} reshape(f32[4]{0:T(128)S(1)} %sqrt.7) | data formatting | bytes 32 | tf_op jit(solution)/shard_map/sqrt | solution.py:772
  (1 shorter events, 0.0 us)
Async XLA Ops:
  2.1 8.5 %collective-permute-start = (f32[3,32,512]{2,1,0:T(8,128)S(1)}, f32[3,32,512]{2,1,0:T(8,128)S(1)}, u32[]{:S(2)}, u32[]{:S(2)}) collective-permute-start(f32[3,32,512]{2,1,0:T(8,128)S(1)} %get-tuple-element.32.sent_a), channel_id=1, source_target_pairs={{0,1},{1,0},{2,3},{3,2},{4,5},{5,4},{6,7},{7,6},{8,9},{9,8},{10,11... | collective-permute-start | bytes 589832 | tf_op jit(solution)/shard_map/ppermute | solution.py:29
  5.4 7.0 %collective-permute-start.1 = (f32[3,32,512]{2,1,0:T(8,128)S(1)}, f32[3,32,512]{2,1,0:T(8,128)S(1)}, u32[]{:S(2)}, u32[]{:S(2)}) collective-permute-start(f32[3,32,512]{2,1,0:T(8,128)S(1)} %get-tuple-element.33.sent_c), channel_id=1, source_target_pairs={{1,2},{2,1},{3,4},{4,3},{5,6},{6,5},{7,8},{8,7},{9,10},{10,9},{11,... | collective-permute-start | bytes 589832 | tf_op jit(solution)/shard_map/ppermute | solution.py:29
  12.9 6.9 %collective-permute-start.2 = (f32[4,112,128]{2,1,0:T(8,128)S(1)}, f32[4,112,128]{2,1,0:T(8,128)S(1)}, u32[]{:S(2)}, u32[]{:S(2)}) collective-permute-start(f32[4,112,128]{2,1,0:T(8,128)S(1)} %get-tuple-element.35), channel_id=1, source_target_pairs={{0,32},{32,0},{64,96},{96,64},{128,160},{160,128},{192,224},{224,1... | collective-permute-start | bytes 688136 | tf_op jit(solution)/shard_map/ppermute | solution.py:29
  13.0 6.8 %collective-permute-start.3 = (f32[4,112,128]{2,1,0:T(8,128)S(1)}, f32[4,112,128]{2,1,0:T(8,128)S(1)}, u32[]{:S(2)}, u32[]{:S(2)}) collective-permute-start(f32[4,112,128]{2,1,0:T(8,128)S(1)} %get-tuple-element.36), channel_id=1, source_target_pairs={{32,64},{64,32},{96,128},{128,96},{160,192},{192,160},{33,65},{65,... | collective-permute-start | bytes 688136 | tf_op jit(solution)/shard_map/ppermute | solution.py:29
